TPU v7x, 32 devices: a whole 2x2x4 slice. The times are simulated.
32 devices in a mesh: member: 2 (over core), tp: 16 (over z, y, x).
Axes of the slice: x: 2, y: 2, z: 4, core: 2. Of those that a mesh axis runs over, the one named last changes fastest.
Arguments:
- stream_in: bfloat16 [512, 4096], P(('member', 'tp')), may hold values from -6 to 6
- kv_cache: bfloat16 [512, 512, 2048], P(('member', 'tp')), may hold values from -400 to 400
- lengths: int32 [128], replicated, may hold values from 1 to 512
- targets: int32 [128], replicated, may hold values from 0 to 65535
- norm_gains: float32 [3, 4096], replicated, may hold values from 0.1 to 1.9
- w_qkv: bfloat16 [4096, 6144], P(None, 'tp'), may hold values from -0.09375 to 0.09375
- w_out: bfloat16 [4096, 4096], P('tp'), may hold values from -0.09375 to 0.09375
- w_gate_up: bfloat16 [2, 4096, 14336], P(None, None, 'tp'), may hold values from -0.09375 to 0.09375
- w_down: bfloat16 [14336, 4096], P('tp'), may hold values from -0.046875 to 0.046875
- lm_head: bfloat16 [4096, 65536], P(None, 'tp'), may hold values from -300 to 300
- fast_in: float32 [4, 2, 4096], P('member'), may hold values from 0.1 to 1.9
- fast_hidden: float32 [4, 3, 14336], P('member', None, 'tp'), may hold values from 0.1 to 1.9
- fast_out: float32 [4, 4096], P('member'), may hold values from 0.1 to 1.9
Outputs:
- mean_logits: bfloat16 [128, 65536], P(None, 'tp')
- token_logprob: float32 [128], replicated
Inputs may be any that keep to these rules, and one draw needn't show every extreme that they name: lengths is the same for all members.
All inputs are finite; a program needn't handle non-finite values.
Results may differ from a plain program's by a relative error of at most 0.02.
Values may be sent and summed in bfloat16 or wider, within the bound.
A program may use at most 192 MiB of HBM per device.

v0:
```python
import functools

import jax
import jax.numpy as jnp
from jax import lax
from jax.experimental import pallas as pl
from jax.experimental.pallas import tpu as pltpu
from jax.sharding import PartitionSpec as P

HEADS = 32
KV = 8
HD = 128
CACHE = 512


ROPE_BASE = 500000.0


def rms_norm(values_in, gain):
    return (
        values_in
        * lax.rsqrt(jnp.mean(values_in * values_in, axis=-1, keepdims=True) + 1e-05)
        * gain
    )


def rotate(values_in, positions):
    half_dim = values_in.shape[-1] // 2
    frequency = ROPE_BASE ** (-jnp.arange(half_dim, dtype=jnp.float32) * 2.0 / values_in.shape[-1])
    angles = positions.astype(jnp.float32)[:, None, None] * frequency[None, None, :]
    lower_half = values_in[..., :half_dim]
    upper_half = values_in[..., half_dim:]
    return jnp.concatenate(
        [
            lower_half * jnp.cos(angles) - upper_half * jnp.sin(angles),
            upper_half * jnp.cos(angles) + lower_half * jnp.sin(angles),
        ],
        axis=-1,
    )


def attend(projected, cache_rows, positions):
    row_count = projected.shape[0]
    head_cols = HEADS * HD
    kv_cols = KV * HD
    queries = rotate(
        projected[:, :head_cols].astype(jnp.float32).reshape(row_count, HEADS, HD), positions
    ).astype(jnp.bfloat16)
    new_key = rotate(
        projected[:, head_cols : head_cols + kv_cols]
        .astype(jnp.float32)
        .reshape(row_count, KV, HD),
        positions,
    ).astype(jnp.bfloat16)
    new_value = projected[:, head_cols + kv_cols :].reshape(row_count, KV, HD)
    cache_keys = cache_rows[:, :, :kv_cols].reshape(row_count, CACHE, KV, HD)
    cache_values = cache_rows[:, :, kv_cols:].reshape(row_count, CACHE, KV, HD)
    grouped = queries.reshape(row_count, KV, HEADS // KV, HD)
    inv_root = HD ** (-0.5)
    cached = (
        jnp.einsum("rkgd,rckd->rkgc", grouped, cache_keys, preferred_element_type=jnp.float32)
        * inv_root
    )
    fresh = (
        jnp.einsum("rkgd,rkd->rkg", grouped, new_key, preferred_element_type=jnp.float32) * inv_root
    )
    in_cache = jnp.arange(CACHE)[None, :] < positions[:, None]
    cached = jnp.where(in_cache[:, None, None, :], cached, -1e30)
    peak = jnp.maximum(jnp.max(cached, axis=-1), fresh)
    weights = jnp.exp(cached - peak[..., None])
    fresh_w = jnp.exp(fresh - peak)
    total_sum = jnp.sum(weights, axis=-1) + fresh_w
    probs = (weights / total_sum[..., None]).astype(jnp.bfloat16)
    fresh_p = (fresh_w / total_sum).astype(jnp.bfloat16)
    result = jnp.einsum("rkgc,rckd->rkgd", probs, cache_values, preferred_element_type=jnp.float32)
    result = (
        result
        + fresh_p.astype(jnp.float32)[..., None] * new_value.astype(jnp.float32)[:, :, None, :]
    )
    return result.reshape(row_count, HEADS * HD).astype(jnp.bfloat16)


def plain_body(
    stream_in,
    kv_cache,
    lengths,
    targets,
    norm_gains,
    w_qkv,
    w_out,
    w_gate_up,
    w_down,
    lm_head,
    fast_in,
    fast_hidden,
    fast_out,
):
    tp_count = lax.axis_size("tp")
    tp_rank = lax.axis_index("tp")
    mem_dev = fast_in.shape[0]
    batch_rows = lengths.shape[0]
    own_rows = stream_in.shape[0]
    all_rows = own_rows * tp_count
    width = stream_in.shape[1]
    first_row = tp_rank * own_rows
    positions = lax.dynamic_slice_in_dim(lengths, first_row % batch_rows, own_rows, 0)
    own_member = first_row // batch_rows
    own_scale = lax.dynamic_index_in_dim(fast_out, own_member, 0, keepdims=True)
    own_normed = rms_norm(stream_in.astype(jnp.float32), norm_gains[0]).astype(jnp.bfloat16)
    attn_in = lax.all_gather(own_normed, "tp", axis=0, tiled=True)
    projected = jnp.dot(attn_in, w_qkv, preferred_element_type=jnp.float32).astype(jnp.bfloat16)
    row_major = lax.all_to_all(projected, "tp", split_axis=0, concat_axis=1, tiled=True)
    attended = attend(row_major, kv_cache, positions)
    head_major = lax.all_to_all(attended, "tp", split_axis=1, concat_axis=0, tiled=True)
    picked = head_major
    attn_sum = lax.psum_scatter(
        jnp.dot(picked, w_out, preferred_element_type=jnp.float32),
        "tp",
        scatter_dimension=0,
        tiled=True,
    )
    middle = (stream_in.astype(jnp.float32) + attn_sum).astype(jnp.bfloat16)
    own_ffn = rms_norm(middle.astype(jnp.float32), norm_gains[1]).astype(jnp.bfloat16)
    ffn_in = lax.all_gather(own_ffn, "tp", axis=0, tiled=True)
    grouped = ffn_in.astype(jnp.float32).reshape(mem_dev, batch_rows, width)
    gate_in = (grouped * fast_in[:, 0][:, None, :]).astype(jnp.bfloat16).reshape(all_rows, width)
    up_in = (grouped * fast_in[:, 1][:, None, :]).astype(jnp.bfloat16).reshape(all_rows, width)
    hidden_cols = w_gate_up.shape[2]
    gate_act = (
        jnp.dot(gate_in, w_gate_up[0], preferred_element_type=jnp.float32).reshape(
            mem_dev, batch_rows, hidden_cols
        )
        * fast_hidden[:, 0][:, None, :]
    )
    up_act = (
        jnp.dot(up_in, w_gate_up[1], preferred_element_type=jnp.float32).reshape(
            mem_dev, batch_rows, hidden_cols
        )
        * fast_hidden[:, 1][:, None, :]
    )
    hidden = (
        (jax.nn.silu(gate_act) * up_act * fast_hidden[:, 2][:, None, :])
        .astype(jnp.bfloat16)
        .reshape(all_rows, hidden_cols)
    )
    picked = hidden
    down_sum = lax.psum_scatter(
        jnp.dot(picked, w_down, preferred_element_type=jnp.float32),
        "tp",
        scatter_dimension=0,
        tiled=True,
    )
    layer_out = (middle.astype(jnp.float32) + down_sum * own_scale).astype(jnp.bfloat16)
    own_final = rms_norm(layer_out.astype(jnp.float32), norm_gains[2]).astype(jnp.bfloat16)
    final_in = lax.all_gather(own_final, "tp", axis=0, tiled=True)
    logits = jnp.dot(final_in, lm_head, preferred_element_type=jnp.float32)
    vocab_cols = lm_head.shape[1]
    member_total = jnp.sum(logits.reshape(mem_dev, batch_rows, vocab_cols), axis=0)
    member_count = mem_dev * lax.axis_size("member")
    mean_logit = (
        lax.psum(member_total.astype(jnp.bfloat16), "member").astype(jnp.float32) / member_count
    )
    column_ids = tp_rank * vocab_cols + jnp.arange(vocab_cols)
    target_part = jnp.sum(
        jnp.where(column_ids[None, :] == targets[:, None], mean_logit, 0.0), axis=-1
    )
    local_peak = jnp.max(mean_logit, axis=-1)
    peak = lax.pmax(local_peak, "tp")
    exp_total, target_logit = lax.psum(
        (jnp.sum(jnp.exp(mean_logit - peak[:, None]), axis=-1), target_part), "tp"
    )
    token_logprob = target_logit - (peak + jnp.log(exp_total))
    return (mean_logit.astype(jnp.bfloat16), token_logprob)


BF16 = jnp.bfloat16
F32 = jnp.float32
DMA = pltpu.SemaphoreType.DMA
QUAD = 4


def norm_rows(values_in, gain):
    return (
        values_in
        * lax.rsqrt(jnp.mean(values_in * values_in, axis=-1, keepdims=True) + 1e-05)
        * gain
    )


class Place:
    def __init__(self, lines):
        self.tp = lax.axis_index("tp")
        self.member = lax.axis_index("member")
        self.lines = lines
        self.quad = lax.rem(self.tp, QUAD)
        self.line = self.tp // QUAD
        self.quad_x = self.quad + 1 - 2 * lax.rem(self.quad, 2)
        self.quad_y = lax.rem(self.quad + 2, QUAD)
        self.quad_d = self.quad_x + self.quad_y - self.quad
        self.to_x = {"tp": self.line * QUAD + self.quad_x}
        self.to_y = {"tp": self.line * QUAD + self.quad_y}

    def line_at(self, step):
        return lax.rem(self.line + step + self.lines, self.lines)

    def to_line(self, step):
        return {"tp": self.line_at(step) * QUAD + self.quad}


def remote(src, dst, send_sem, recv_sem, device):
    copy = pltpu.make_async_remote_copy(
        src_ref=src,
        dst_ref=dst,
        send_sem=send_sem,
        recv_sem=recv_sem,
        device_id=device,
        device_id_type=pl.DeviceIdType.MESH,
    )
    copy.start()
    return copy


def greet(devices):
    barrier = pltpu.get_barrier_semaphore()
    for device in devices:
        pl.semaphore_signal(
            barrier, inc=1, device_id=device, device_id_type=pl.DeviceIdType.MESH
        )
    pl.semaphore_wait(barrier, len(devices))


def gather_rows(place, own, out, sems, line_steps, block_of):
    local_sem, sends, recvs = sems
    rows, cols = own.shape
    half = cols // 2

    def rows_of(step, quad):
        return pl.ds(pl.multiple_of(block_of(step, quad) * rows, rows), rows)

    mine = out.at[rows_of(0, place.quad)]
    local = pltpu.make_async_copy(own, mine, local_sem)
    local.start()
    line_copies = []
    for k, step in enumerate(line_steps):
        if k:
            line_copies.append(
                remote(own, mine, sends.at[0, k], recvs.at[0, k], place.to_line(step))
            )
        else:
            line_copies.append(None)
    by_x, by_y, over_x, over_y = [], [], [], []

    def spread(k):
        block = own if k == 0 else out.at[rows_of(-line_steps[k], place.quad)]
        into = out.at[rows_of(-line_steps[k], place.quad)]
        by_x.append(remote(block, into, sends.at[1, k], recvs.at[1, k], place.to_x))
        by_y.append(remote(block, into, sends.at[2, k], recvs.at[2, k], place.to_y))

    def relay(k):
        by_x[k].wait_recv()
        from_x = out.at[rows_of(-line_steps[k], place.quad_x), pl.ds(0, half)]
        over_y.append(remote(from_x, from_x, sends.at[3, k], recvs.at[3, k], place.to_y))
        by_y[k].wait_recv()
        from_y = out.at[rows_of(-line_steps[k], place.quad_y), pl.ds(half, half)]
        over_x.append(remote(from_y, from_y, sends.at[4, k], recvs.at[4, k], place.to_x))

    spread(0)
    for k in range(1, len(line_steps)):
        line_copies[k].wait_recv()
        spread(k)
        relay(k - 1)
    relay(len(line_steps) - 1)
    for k in range(len(line_steps)):
        over_y[k].wait_recv()
        over_x[k].wait_recv()
    local.wait()
    for copies in (line_copies, by_x, by_y, over_x, over_y):
        for copy in copies:
            if copy is not None:
                copy.wait_send()


def sum_rows(place, part, sems, bufs):
    sends, recvs = sems
    got_dx, got_dy, put_x, put_y, got_x, got_y, put_z, got_z = bufs
    rows = got_x.shape[1]
    half = got_dx.shape[2]
    low, high = pl.ds(0, half), pl.ds(half, half)
    steps = list(range(1, place.lines)) + [0]

    def rows_of(step, quad):
        index = place.line_at(step) * QUAD + quad
        return pl.ds(pl.multiple_of(index * rows, rows), rows)

    d_x, d_y, x_high, y_low, x_low, y_high, z_copies = {}, {}, {}, {}, {}, {}, {}
    for k in steps:
        diag = rows_of(k, place.quad_d)
        d_x[k] = remote(part.at[diag, high], got_dx.at[k], sends.at[0, k], recvs.at[0, k], place.to_x)
        d_y[k] = remote(part.at[diag, low], got_dy.at[k], sends.at[1, k], recvs.at[1, k], place.to_y)
    for k in steps:
        x_high[k] = remote(
            part.at[rows_of(k, place.quad_x), high], got_x.at[k, :, high],
            sends.at[2, k], recvs.at[2, k], place.to_x,
        )
        y_low[k] = remote(
            part.at[rows_of(k, place.quad_y), low], got_y.at[k, :, low],
            sends.at[3, k], recvs.at[3, k], place.to_y,
        )
        d_y[k].wait_recv()
        put_x[k] = (
            part[rows_of(k, place.quad_x), low].astype(F32) + got_dy[k].astype(F32)
        ).astype(BF16)
        x_low[k] = remote(
            put_x.at[k], got_x.at[k, :, low], sends.at[4, k], recvs.at[4, k], place.to_x
        )
        d_x[k].wait_recv()
        put_y[k] = (
            part[rows_of(k, place.quad_y), high].astype(F32) + got_dx[k].astype(F32)
        ).astype(BF16)
        y_high[k] = remote(
            put_y.at[k], got_y.at[k, :, high], sends.at[5, k], recvs.at[5, k], place.to_y
        )
    total = None
    for k in steps:
        for copies in (x_high, y_low, x_low, y_high):
            copies[k].wait_recv()
        quad_sum = (
            part[rows_of(k, place.quad), :].astype(F32)
            + got_x[k].astype(F32)
            + got_y[k].astype(F32)
        )
        if k:
            put_z[k] = quad_sum.astype(BF16)
            z_copies[k] = remote(
                put_z.at[k], got_z.at[k], sends.at[6, k], recvs.at[6, k], place.to_line(k)
            )
        else:
            total = quad_sum
    for k in steps[:-1]:
        z_copies[k].wait_recv()
        total = total + got_z[k].astype(F32)
    for copies in (d_x, d_y, x_high, y_low, x_low, y_high, z_copies):
        for copy in copies.values():
            copy.wait_send()
    return total


def near(place):
    return [place.to_x, place.to_y] + [place.to_line(k) for k in range(1, place.lines)]


def gather_kernel(lines, stream, gain, out, own, local_sem, sends, recvs):
    place = Place(lines)
    own[...] = norm_rows(stream[...].astype(F32), gain[...]).astype(BF16)
    greet(near(place))
    gather_rows(
        place, own, out, (local_sem, sends, recvs), list(range(lines)),
        lambda step, quad: place.line_at(step) * QUAD + quad,
    )


def tail_kernel(
    lines, heads_in, w_out, stream, gains, fast_in, fast_hidden, scale, targets, w_gate_up, w_down, lm_head,
    out, logprob,
    part, middle, ffn_in, acts, hidden, gate_up, down, words, own, half_own, away, from_core,
    pair, from_pair, mean, rows_in, stats, table,
    load_sems, tile_sends, tile_recvs, stat_sends, stat_recvs, side_sends, side_recvs,
    local_sem, sends, recvs, last_sem, last_sends, last_recvs, *sums
):
    place = Place(lines)
    tp_count = lines * QUAD
    member = place.member
    cols = words.shape[1]
    other = {"member": 1 - member}
    loads = [
        pltpu.make_async_copy(w_gate_up, gate_up, load_sems.at[0]),
        pltpu.make_async_copy(w_down, down, load_sems.at[1]),
        pltpu.make_async_copy(
            lm_head.at[:, pl.ds(pl.multiple_of(member * cols, cols), cols)], words, load_sems.at[2]
        ),
    ]
    for load in loads:
        load.start()
    others = []
    for core in (member, 1 - member):
        for step in range(tp_count):
            if others or step:
                others.append({"member": core, "tp": lax.rem(place.tp + step, tp_count)})
    greet(others)
    wide = 512

    @pl.loop(0, part.shape[1] // wide)
    def _(i):
        span = pl.ds(pl.multiple_of(i * wide, wide), wide)
        part[:, span] = jnp.dot(
            heads_in[...], w_out[:, span], preferred_element_type=F32
        ).astype(BF16)

    count = len(sums) // 2
    total = sum_rows(place, part, sums[:2], sums[2:count])
    middle[...] = (stream[...].astype(F32) + total).astype(BF16)
    own[...] = norm_rows(middle[...].astype(F32), gains[1][:1]).astype(BF16)
    gather_rows(
        place, own, ffn_in, (local_sem, sends, recvs), list(range(lines)),
        lambda step, quad: place.line_at(step) * QUAD + quad,
    )
    loads[0].wait()
    members = fast_in.shape[0]
    batch_rows = ffn_in.shape[0] // members
    acts[...] = jnp.zeros_like(acts)

    @pl.loop(0, ffn_in.shape[1] // wide)
    def _(i):
        span = pl.ds(pl.multiple_of(i * wide, wide), wide)
        values = ffn_in[:, span].astype(F32)
        for j in range(2):
            scaled = jnp.concatenate(
                [
                    values[m * batch_rows : (m + 1) * batch_rows] * fast_in[m, j, :, span][:1]
                    for m in range(members)
                ],
                axis=0,
            ).astype(BF16)
            acts[j] += jnp.dot(scaled, gate_up[j, span, :], preferred_element_type=F32)

    for m in range(members):
        rows = slice(m * batch_rows, (m + 1) * batch_rows)
        gate = acts[0, rows, :] * fast_hidden[m, 0][:1]
        hidden[rows, :] = (
            gate / (1.0 + jnp.exp(-gate))
            * (acts[1, rows, :] * fast_hidden[m, 1][:1])
            * fast_hidden[m, 2][:1]
        ).astype(BF16)
    loads[1].wait()

    @pl.loop(0, part.shape[1] // wide)
    def _(i):
        span = pl.ds(pl.multiple_of(i * wide, wide), wide)
        part[:, span] = jnp.dot(
            hidden[...], down[:, span], preferred_element_type=F32
        ).astype(BF16)

    total = sum_rows(place, part, sums[count : count + 2], sums[count + 2 :])
    layer_out = (middle[...].astype(F32) + total * scale[...]).astype(BF16)
    normed = norm_rows(layer_out.astype(F32), gains[2][:1]).astype(BF16)
    half = mean.shape[1]
    first = member == 0
    low, high = normed[:, :half].astype(F32), normed[:, half:].astype(F32)
    half_own[...] = jnp.where(first, low, high)
    away[...] = jnp.where(first, high, low).astype(BF16)
    core = remote(away, from_core, side_sends.at[0], side_recvs.at[0], other)
    core.wait_recv()
    half_own[...] = half_own[...] + from_core[...].astype(F32)
    pair[...] = half_own[...]
    twin = remote(
        pair, from_pair, side_sends.at[1], side_recvs.at[1], place.to_line(lines // 2)
    )
    twin.wait_recv()
    mean[...] = ((half_own[...] + from_pair[...]) * 0.25).astype(BF16)
    turn = 1 - 2 * lax.rem(place.line, 2)

    class Pairwise:
        pass

    near_line = Pairwise()
    near_line.quad, near_line.quad_x, near_line.quad_y = place.quad, place.quad_x, place.quad_y
    near_line.to_x, near_line.to_y = place.to_x, place.to_y
    near_line.to_line = lambda step: {"tp": (place.line + turn) * QUAD + place.quad}
    mine = rows_in.at[member]
    gather_rows(
        near_line, mean, mine, (last_sem, last_sends, last_recvs), [0, 1],
        lambda step, quad: lax.rem(place.line + abs(step), 2) * QUAD + quad,
    )
    share = remote(mine, mine, side_sends.at[2], side_recvs.at[2], other)
    loads[2].wait()
    share.wait_recv()
    tile_width = cols // tile_sends.shape[0]
    batch = rows_in.shape[1]
    peak = jnp.full((batch, 1), -jnp.inf, F32)
    amount = jnp.zeros((batch, 1), F32)
    found = jnp.zeros((batch, 1), F32)
    tiles = []
    for i in range(tile_sends.shape[0]):
        span = pl.ds(i * tile_width, tile_width)
        tile = jnp.dot(rows_in[0], words[:half, span], preferred_element_type=F32) + jnp.dot(
            rows_in[1], words[half:, span], preferred_element_type=F32
        )
        into = out.at[:, pl.ds(pl.multiple_of(member * cols + i * tile_width, tile_width), tile_width)]
        into[...] = tile.astype(BF16)
        tiles.append(remote(into, into, tile_sends.at[i], tile_recvs.at[i], other))
        new = jnp.maximum(peak, jnp.max(tile, axis=-1, keepdims=True))
        amount = amount * jnp.exp(peak - new) + jnp.sum(
            jnp.exp(tile - new), axis=-1, keepdims=True
        )
        peak = new
        column = (
            (place.tp * 2 + member) * cols
            + i * tile_width
            + lax.broadcasted_iota(jnp.int32, tile.shape, 1)
        )
        found = found + jnp.sum(
            jnp.where(column == targets[...], tile, 0.0), axis=-1, keepdims=True
        )
    lane = lax.broadcasted_iota(jnp.int32, (batch, 128), 1)
    block = jnp.where(lane == 0, peak, jnp.where(lane == 1, amount, found))
    stats[...] = jnp.transpose(block)[:8, :]
    copies = []
    for slot, device in enumerate(others):
        copies.append(
            remote(stats, table.at[slot + 1], stat_sends.at[slot], stat_recvs.at[slot], device)
        )
    table[0] = stats[...]
    for copy in copies:
        copy.wait_recv()
    top = jnp.max(table[:, 0, :], axis=0, keepdims=True)
    amount = jnp.sum(table[:, 1, :] * jnp.exp(table[:, 0, :] - top), axis=0, keepdims=True)
    found = jnp.sum(table[:, 2, :], axis=0, keepdims=True)
    logprob[...] = found - (top + jnp.log(amount))
    for copy in tiles:
        copy.wait_recv()
    for copy in [core, twin, share] + tiles + copies:
        copy.wait_send()


VMEM = pl.BlockSpec(memory_space=pltpu.VMEM)
ANY = pl.BlockSpec(memory_space=pl.ANY)
MIB = 1024 * 1024


def call_linked(kernel, number, out_shape, scratch, args, mib, far=0):
    return pl.pallas_call(
        kernel,
        out_shape=out_shape,
        in_specs=[VMEM] * (len(args) - far) + [ANY] * far,
        out_specs=jax.tree.map(lambda _: VMEM, out_shape),
        scratch_shapes=scratch,
        compiler_params=pltpu.CompilerParams(
            collective_id=number, has_side_effects=True, vmem_limit_bytes=mib * MIB
        ),
        cost_estimate=pl.CostEstimate(flops=0, bytes_accessed=64 * MIB, transcendentals=0),
    )(*args)


def gather_scratch(lines):
    return [DMA, DMA((5, lines)), DMA((5, lines))]


def sum_scratch(lines, rows, cols):
    small = pltpu.VMEM((lines, rows, cols // 2), BF16)
    large = pltpu.VMEM((lines, rows, cols), BF16)
    return [DMA((7, lines)), DMA((7, lines)), small, small, small, small, large, large, large, large]


def attend_kernel(positions, query, fresh_key, fresh_value, cache, out):
    row = pl.program_id(0)
    heads, head_size = query.shape[1], query.shape[2]
    kv_cols = cache.shape[2] // 2
    key_heads = kv_cols // head_size
    group = heads // key_heads
    count = cache.shape[1]
    query_row = query[0].astype(F32)
    inv_root = head_size ** (-0.5)
    wide = jnp.concatenate([query_row] * key_heads, axis=1)
    owner = lax.broadcasted_iota(jnp.int32, wide.shape, 0) // group
    column = lax.broadcasted_iota(jnp.int32, wide.shape, 1) // head_size
    wide = jnp.where(owner == column, wide, 0.0).astype(BF16)
    scores = (
        lax.dot_general(
            wide, cache[0, :, :kv_cols], (((1,), (1,)), ((), ())), preferred_element_type=F32
        )
        * inv_root
    )
    spot = lax.broadcasted_iota(jnp.int32, scores.shape, 1)
    scores = jnp.where(spot < positions[row], scores, -1e30)
    fresh = jnp.sum(query_row * fresh_key[0].astype(F32), axis=-1, keepdims=True) * inv_root
    peak = jnp.maximum(jnp.max(scores, axis=-1, keepdims=True), fresh)
    weights = jnp.exp(scores - peak)
    fresh_w = jnp.exp(fresh - peak)
    total_sum = jnp.sum(weights, axis=-1, keepdims=True) + fresh_w
    probs = (weights / total_sum).astype(BF16)
    fresh_p = (fresh_w / total_sum).astype(BF16).astype(F32)
    full = jnp.dot(probs, cache[0, :, kv_cols:], preferred_element_type=F32)
    full = jnp.where(owner == column, full, 0.0)
    result = full[:, :head_size]
    for k in range(1, key_heads):
        result = result + full[:, k * head_size : (k + 1) * head_size]
    out[0] = (result + fresh_p * fresh_value[0].astype(F32)).astype(BF16)


def attend_rows(projected, cache_rows, positions):
    rows = projected.shape[0]
    head_cols, kv_cols = HEADS * HD, KV * HD
    group = HEADS // KV
    queries = rotate(
        projected[:, :head_cols].astype(F32).reshape(rows, HEADS, HD), positions
    ).astype(BF16)
    new_key = rotate(
        projected[:, head_cols : head_cols + kv_cols].astype(F32).reshape(rows, KV, HD), positions
    ).astype(BF16)
    new_value = projected[:, head_cols + kv_cols :].reshape(rows, KV, HD)
    new_key = jnp.repeat(new_key, group, axis=1)
    new_value = jnp.repeat(new_value, group, axis=1)
    per_row = pl.BlockSpec((1, HEADS, HD), lambda r, p: (r, 0, 0))
    cache_spec = pl.BlockSpec((1,) + cache_rows.shape[1:], lambda r, p: (r, 0, 0))
    result = pl.pallas_call(
        attend_kernel,
        grid_spec=pltpu.PrefetchScalarGridSpec(
            num_scalar_prefetch=1,
            grid=(rows,),
            in_specs=[per_row, per_row, per_row, cache_spec],
            out_specs=per_row,
        ),
        out_shape=jax.ShapeDtypeStruct((rows, HEADS, HD), BF16),
        compiler_params=pltpu.CompilerParams(vmem_limit_bytes=32 * 1024 * 1024),
    )(positions, queries, new_key, new_value, cache_rows)
    return result.reshape(rows, head_cols)


def whole_tiles(rows):
    return jnp.broadcast_to(rows[..., None, :], rows.shape[:-1] + (8, rows.shape[-1]))


def linked_body(
    stream_in,
    kv_cache,
    lengths,
    targets,
    norm_gains,
    w_qkv,
    w_out,
    w_gate_up,
    w_down,
    lm_head,
    fast_in,
    fast_hidden,
    fast_out,
):
    tp_count = lax.axis_size("tp")
    tp_rank = lax.axis_index("tp")
    lines = tp_count // QUAD
    batch_rows = lengths.shape[0]
    own_rows, width = stream_in.shape
    all_rows = own_rows * tp_count
    first_row = tp_rank * own_rows
    positions = lax.dynamic_slice_in_dim(lengths, first_row % batch_rows, own_rows, 0)
    own_member = first_row // batch_rows
    own_scale = lax.dynamic_index_in_dim(fast_out, own_member, 0, keepdims=True)
    all_shape = jax.ShapeDtypeStruct((all_rows, width), BF16)
    own_buf = pltpu.VMEM((own_rows, width), BF16)

    attn_in = call_linked(
        functools.partial(gather_kernel, lines), 1, all_shape,
        [own_buf] + gather_scratch(lines), (stream_in, norm_gains[0:1]), 16,
    )
    projected = jnp.dot(attn_in, w_qkv, preferred_element_type=F32).astype(BF16)
    row_major = lax.all_to_all(projected, "tp", split_axis=0, concat_axis=1, tiled=True)
    attended = attend_rows(row_major, kv_cache, positions)
    head_major = lax.all_to_all(attended, "tp", split_axis=1, concat_axis=0, tiled=True)
    half = width // 2
    devices = 2 * tp_count
    vocab_cols = lm_head.shape[1]
    tiles = 4
    mean_logits, logprob = call_linked(
        functools.partial(tail_kernel, lines), 2,
        [
            jax.ShapeDtypeStruct((batch_rows, vocab_cols), BF16),
            jax.ShapeDtypeStruct((1, batch_rows), F32),
        ],
        [
            pltpu.VMEM((all_rows, width), BF16),
            own_buf,
            pltpu.VMEM((all_rows, width), BF16),
            pltpu.VMEM((2, all_rows, w_gate_up.shape[2]), F32),
            pltpu.VMEM((all_rows, w_gate_up.shape[2]), BF16),
            pltpu.VMEM(w_gate_up.shape, BF16),
            pltpu.VMEM(w_down.shape, BF16),
            pltpu.VMEM((width, vocab_cols // 2), BF16),
            own_buf,
            pltpu.VMEM((own_rows, half), F32),
            pltpu.VMEM((own_rows, half), BF16),
            pltpu.VMEM((own_rows, half), BF16),
            pltpu.VMEM((own_rows, half), F32),
            pltpu.VMEM((own_rows, half), F32),
            pltpu.VMEM((own_rows, half), BF16),
            pltpu.VMEM((2, batch_rows, half), BF16),
            pltpu.VMEM((8, batch_rows), F32),
            pltpu.VMEM((devices, 8, batch_rows), F32),
            DMA((3,)), DMA((tiles,)), DMA((tiles,)), DMA((devices,)), DMA((devices,)), DMA((3,)), DMA((3,)),
        ]
        + gather_scratch(lines)
        + gather_scratch(2)
        + sum_scratch(lines, own_rows, width)
        + sum_scratch(lines, own_rows, width),
        (
            head_major, w_out, stream_in, whole_tiles(norm_gains), whole_tiles(fast_in),
            whole_tiles(fast_hidden), own_scale, targets[:, None],
            w_gate_up, w_down, lm_head,
        ),
        58, 3,
    )
    return (mean_logits, logprob[0])


def body(*args):
    stream_in, lengths, fast_in = args[0], args[2], args[10]
    tp_count = lax.axis_size("tp")
    lines = tp_count // QUAD
    full_rows = stream_in.shape[0] % 16 == 0
    two_halves = lax.axis_size("member") == 2 and fast_in.shape[0] == 2
    even_lines = tp_count % QUAD == 0 and lines % 4 == 0
    pairs = stream_in.shape[0] * tp_count == 2 * lengths.shape[0] and lines == 4
    if full_rows and two_halves and even_lines and pairs:
        return linked_body(*args)
    return plain_body(*args)


def solution(mesh):
    in_specs = (
        P(("member", "tp"), None),
        P(("member", "tp"), None, None),
        P(),
        P(),
        P(),
        P(None, "tp"),
        P("tp", None),
        P(None, None, "tp"),
        P("tp", None),
        P(None, "tp"),
        P("member", None, None),
        P("member", None, "tp"),
        P("member", None),
    )
    out_specs = (P(None, "tp"), P())
    return jax.shard_map(body, mesh=mesh, in_specs=in_specs, out_specs=out_specs, check_vma=False)
```

profile of v0, /device:TPU:0, one launch (start us, length us, event | category | flops | bytes accessed | tf_op | source)
XLA Modules:
  0.0 208.0 jit_solution(6020488717692503884)
XLA Ops:
  0.6 0.0 copy-start
  0.6 1.0 slice.24.gain
  1.7 0.0 copy-start.2
  1.7 0.9 copy-done.2
  2.6 29.0 %shard_map.140 = bf16[256,4096]{1,0:T(8,128)(2,1)S(1)} custom-call(bf16[16,4096]{1,0:T(8,128)(2,1)S(1)} %copy-done.2, f32[1,4096]{1,0:T(1,128)S(1)} %slice.24.gain), custom_call_target="tpu_custom_call" | custom-call | bytes 67108864 | tf_op jit(solution)/shard_map/pallas_call | solution.py:531
  31.6 0.0 copy-start.6
  31.6 0.0 copy-start.8
  31.6 0.0 copy-start.9
  31.7 2.0 convolution_convert_fusion
  33.6 7.1 %all-to-all-start = ((bf16[16,16,384]{2,1,0:T(8,128)(2,1)}), bf16[16,16,384]{2,1,0:T(8,128)(2,1)S(1)}, u32[]{:S(2)}, u32[]{:S(2)}) async-start(bf16[16,16,384]{2,1,0:T(8,128)(2,1)} %bitcast), calls=%async_computation | async-start | bytes 393216 | tf_op jit(solution)/shard_map/all_to_all | solution.py:656
  40.8 0.7 copy.18.targets
  41.5 0.1 fusion
  41.6 0.1 multiply_cosine_fusion
  41.7 7.1 %all-to-all-done = bf16[16,16,384]{2,1,0:T(8,128)(2,1)S(1)} async-done(((bf16[16,16,384]{2,1,0:T(8,128)(2,1)}), bf16[16,16,384]{2,1,0:T(8,128)(2,1)S(1)}, u32[]{:S(2)}, u32[]{:S(2)}) %all-to-all-start) | async-done | bytes 196640 | tf_op jit(solution)/shard_map/all_to_all | solution.py:656
  48.9 0.1 copy.20
  48.9 0.1 subtract_convert_fusion.1
  49.0 0.1 subtract_convert_fusion
  49.2 0.1 pad_maximum_fusion.1
  49.3 0.1 pad_maximum_fusion.query
  49.5 0.0 copy-start.7
  49.5 0.0 copy-start.4
  49.5 21.8 %shard_map.141 = bf16[16,32,128]{2,1,0:T(8,128)(2,1)S(1)} custom-call(s32[16]{0:T(128)S(1)} %get-tuple-element.7.positions, bf16[16,32,128]{2,1,0:T(8,128)(2,1)S(1)} %pad_maximum_fusion.query, bf16[16,32,128]{2,1,0:T(8,128)(2,1)S(1)} %bitcast.22, bf16[16,32,128]{2,1,0:T(8,128)(2,1)S(1)} %bitcast.23, bf16[16,512,2048]{2,1,0:T(8,128)(2,1)} %cache.1), custom_call_target="tpu_custom_call" | custom-call | tf_op jit(solution)/shard_map/pallas_call | solution.py:605
  71.4 0.7 copy.16
  72.1 3.5 %all-to-all-start.1 = ((bf16[16,16,256]{2,0,1:T(8,128)(2,1)}), bf16[16,16,256]{2,0,1:T(8,128)(2,1)S(1)}, u32[]{:S(2)}, u32[]{:S(2)}) async-start(bf16[16,16,256]{2,0,1:T(8,128)(2,1)} %copy.16), calls=%async_computation.1 | async-start | bytes 262144 | tf_op jit(solution)/shard_map/all_to_all | solution.py:658
  75.7 0.6 constant_dynamic-slice_fusion.scale
  76.3 7.1 %all-to-all-done.1 = bf16[16,16,256]{2,0,1:T(8,128)(2,1)S(1)} async-done(((bf16[16,16,256]{2,0,1:T(8,128)(2,1)}), bf16[16,16,256]{2,0,1:T(8,128)(2,1)S(1)}, u32[]{:S(2)}, u32[]{:S(2)}) %all-to-all-start.1) | async-done | bytes 131104 | tf_op jit(solution)/shard_map/all_to_all | solution.py:658
  83.4 0.8 broadcast_in_dim.15.fast_in
  84.3 0.8 broadcast_in_dim.14.gains
  85.1 0.7 broadcast_in_dim.16.fast_hidden
  85.7 118.9 %shard_map.142 = (bf16[128,4096]{1,0:T(8,128)(2,1)}, f32[1,128]{1,0:T(1,128)}) custom-call(bf16[256,256]{1,0:T(8,128)(2,1)} %bitcast.29, bf16[256,4096]{1,0:T(8,128)(2,1)} %w_out.1, bf16[16,4096]{1,0:T(8,128)(2,1)} %stream.3, f32[3,8,4096]{2,1,0:T(8,128)} %broadcast_in_dim.14.gains, f32[2,2,8,4096]{3,2,1,0:T(8,128)} %broadcast_in_dim.15.fast_in, ...), custom_call_target="tpu_custom_call" | custom-call | bytes 67108864 | tf_op jit(solution)/shard_map/pallas_call | solution.py:531
  204.6 2.3 %copy.25 = bf16[128,4096]{1,0:T(8,128)(2,1)} copy(bf16[128,4096]{1,0:T(8,128)(2,1)} %get-tuple-element.18) | data formatting | bytes 2097152
  206.9 1.2 copy.26
  (22 shorter events, 0.2 us)
Async XLA Ops:
  0.6 31.0 %copy-start = (bf16[4096,384]{1,0:T(8,128)(2,1)S(1)}, bf16[4096,384]{1,0:T(8,128)(2,1)}, u32[]{:S(2)}) copy-start(bf16[4096,384]{1,0:T(8,128)(2,1)} %param.18) | copy-start | bytes 9437188
  1.7 0.9 copy-start.2
  31.6 9.1 %copy-start.6 = (f32[2,3,896]{2,0,1:T(2,128)S(1)}, f32[2,3,896]{2,0,1:T(2,128)}, u32[]{:S(2)}) copy-start(f32[2,3,896]{2,0,1:T(2,128)} %param.24) | copy-start | bytes 64516
  31.6 9.1 %copy-start.8 = (s32[128]{0:T(128)S(1)}, s32[128]{0:T(128)}, u32[]{:S(2)}) copy-start(s32[128]{0:T(128)} %param.16) | copy-start | bytes 1540
  31.6 9.9 %copy-start.9 = (s32[128]{0:T(128)S(1)}, s32[128]{0:T(128)}, u32[]{:S(2)}) copy-start(s32[128]{0:T(128)} %param.15) | copy-start | bytes 1540
  33.6 15.2 %all-to-all-start = ((bf16[16,16,384]{2,1,0:T(8,128)(2,1)}), bf16[16,16,384]{2,1,0:T(8,128)(2,1)S(1)}, u32[]{:S(2)}, u32[]{:S(2)}) async-start(bf16[16,16,384]{2,1,0:T(8,128)(2,1)} %bitcast), calls=%async_computation | async-start | bytes 393216 | tf_op jit(solution)/shard_map/all_to_all | solution.py:656
  49.5 26.1 %copy-start.7 = (f32[2,4096]{1,0:T(2,128)S(1)}, f32[2,4096]{1,0:T(2,128)}, u32[]{:S(2)}) copy-start(f32[2,4096]{1,0:T(2,128)} %param.25) | copy-start | bytes 98308
  49.5 33.9 %copy-start.5 = (f32[2,2,4096]{2,1,0:T(2,128)S(1)}, f32[2,2,4096]{2,1,0:T(2,128)}, u32[]{:S(2)}) copy-start(f32[2,2,4096]{2,1,0:T(2,128)} %param.23) | copy-start | bytes 196612
  49.5 34.7 %copy-start.4 = (f32[3,4096]{1,0:T(4,128)S(1)}, f32[3,4096]{1,0:T(4,128)}, u32[]{:S(2)}) copy-start(f32[3,4096]{1,0:T(4,128)} %param.17) | copy-start | bytes 147460
  72.1 11.3 %all-to-all-start.1 = ((bf16[16,16,256]{2,0,1:T(8,128)(2,1)}), bf16[16,16,256]{2,0,1:T(8,128)(2,1)S(1)}, u32[]{:S(2)}, u32[]{:S(2)}) async-start(bf16[16,16,256]{2,0,1:T(8,128)(2,1)} %copy.16), calls=%async_computation.1 | async-start | bytes 262144 | tf_op jit(solution)/shard_map/all_to_all | solution.py:658
  83.4 2.3 %copy-start.3 = (bf16[16,16,256]{2,0,1:T(8,128)(2,1)}, bf16[16,16,256]{2,0,1:T(8,128)(2,1)S(1)}, u32[]{:S(2)}) copy-start(bf16[16,16,256]{2,0,1:T(8,128)(2,1)S(1)} %all-to-all-done.1) | copy-start | bytes 393220
  85.7 122.3 %copy-start.1 = (bf16[4096,384]{1,0:T(8,128)(2,1)S(1)}, bf16[4096,384]{1,0:T(8,128)(2,1)}, u32[]{:S(2)}) copy-start(bf16[4096,384]{1,0:T(8,128)(2,1)} %param.18) | copy-start | bytes 9437188
where the time goes:
time: 209 us; the launch traced here: 208 us
  Pallas kernels  170 us (81%)
  waiting for transfers between devices  14.2 us (7%)
  starting transfers between devices  10.6 us (5%)
  local copies, waits for them, and re-layouts  10 us (5%)
    pallas_call x2, Pallas kernels, call_linked(): pl.pallas_call(kernel, out_shape=out_shape, in_specs=[VMEM] * (len(args)...  148 us
    pallas_call x1, Pallas kernels, attend_rows(): pl.pallas_call(attend_kernel, grid_spec=pltpu.PrefetchScalarGridSpec(num_...  21.8 us
    all_to_all x1, waiting for transfers between devices, linked_body(): lax.all_to_all(attended, 'tp', split_axis=1, concat_axis=0, tiled=True)  7.13 us
    all_to_all x1, starting transfers between devices, linked_body(): lax.all_to_all(projected, 'tp', split_axis=0, concat_axis=1, tiled=True)  7.07 us
    all_to_all x1, waiting for transfers between devices, linked_body(): lax.all_to_all(projected, 'tp', split_axis=0, concat_axis=1, tiled=True)  7.07 us
    unnamed x26, local copies, waits for them, and re-layouts  4.5 us
  transfers between devices with their start and end apart: 2, of which 2 were waited for; matrix products, arithmetic and copies ran while one was open for 1% of the time, Pallas kernels for 0%

commit v1 on v0

v1 whole, which is shorter than its diff:
```python
import functools
from types import SimpleNamespace

import jax
import jax.numpy as jnp
from jax import lax
from jax.experimental import pallas as pl
from jax.experimental.pallas import tpu as pltpu
from jax.sharding import PartitionSpec as P

HEADS = 32
KV = 8
HD = 128
CACHE = 512


ROPE_BASE = 500000.0


def rms_norm(values_in, gain):
    return (
        values_in
        * lax.rsqrt(jnp.mean(values_in * values_in, axis=-1, keepdims=True) + 1e-05)
        * gain
    )


def rotate(values_in, positions):
    half_dim = values_in.shape[-1] // 2
    frequency = ROPE_BASE ** (-jnp.arange(half_dim, dtype=jnp.float32) * 2.0 / values_in.shape[-1])
    angles = positions.astype(jnp.float32)[:, None, None] * frequency[None, None, :]
    lower_half = values_in[..., :half_dim]
    upper_half = values_in[..., half_dim:]
    return jnp.concatenate(
        [
            lower_half * jnp.cos(angles) - upper_half * jnp.sin(angles),
            upper_half * jnp.cos(angles) + lower_half * jnp.sin(angles),
        ],
        axis=-1,
    )


def attend(projected, cache_rows, positions):
    row_count = projected.shape[0]
    head_cols = HEADS * HD
    kv_cols = KV * HD
    queries = rotate(
        projected[:, :head_cols].astype(jnp.float32).reshape(row_count, HEADS, HD), positions
    ).astype(jnp.bfloat16)
    new_key = rotate(
        projected[:, head_cols : head_cols + kv_cols]
        .astype(jnp.float32)
        .reshape(row_count, KV, HD),
        positions,
    ).astype(jnp.bfloat16)
    new_value = projected[:, head_cols + kv_cols :].reshape(row_count, KV, HD)
    cache_keys = cache_rows[:, :, :kv_cols].reshape(row_count, CACHE, KV, HD)
    cache_values = cache_rows[:, :, kv_cols:].reshape(row_count, CACHE, KV, HD)
    grouped = queries.reshape(row_count, KV, HEADS // KV, HD)
    inv_root = HD ** (-0.5)
    cached = (
        jnp.einsum("rkgd,rckd->rkgc", grouped, cache_keys, preferred_element_type=jnp.float32)
        * inv_root
    )
    fresh = (
        jnp.einsum("rkgd,rkd->rkg", grouped, new_key, preferred_element_type=jnp.float32) * inv_root
    )
    in_cache = jnp.arange(CACHE)[None, :] < positions[:, None]
    cached = jnp.where(in_cache[:, None, None, :], cached, -1e30)
    peak = jnp.maximum(jnp.max(cached, axis=-1), fresh)
    weights = jnp.exp(cached - peak[..., None])
    fresh_w = jnp.exp(fresh - peak)
    total_sum = jnp.sum(weights, axis=-1) + fresh_w
    probs = (weights / total_sum[..., None]).astype(jnp.bfloat16)
    fresh_p = (fresh_w / total_sum).astype(jnp.bfloat16)
    result = jnp.einsum("rkgc,rckd->rkgd", probs, cache_values, preferred_element_type=jnp.float32)
    result = (
        result
        + fresh_p.astype(jnp.float32)[..., None] * new_value.astype(jnp.float32)[:, :, None, :]
    )
    return result.reshape(row_count, HEADS * HD).astype(jnp.bfloat16)


def plain_body(
    stream_in,
    kv_cache,
    lengths,
    targets,
    norm_gains,
    w_qkv,
    w_out,
    w_gate_up,
    w_down,
    lm_head,
    fast_in,
    fast_hidden,
    fast_out,
):
    tp_count = lax.axis_size("tp")
    tp_rank = lax.axis_index("tp")
    mem_dev = fast_in.shape[0]
    batch_rows = lengths.shape[0]
    own_rows = stream_in.shape[0]
    all_rows = own_rows * tp_count
    width = stream_in.shape[1]
    first_row = tp_rank * own_rows
    positions = lax.dynamic_slice_in_dim(lengths, first_row % batch_rows, own_rows, 0)
    own_member = first_row // batch_rows
    own_scale = lax.dynamic_index_in_dim(fast_out, own_member, 0, keepdims=True)
    own_normed = rms_norm(stream_in.astype(jnp.float32), norm_gains[0]).astype(jnp.bfloat16)
    attn_in = lax.all_gather(own_normed, "tp", axis=0, tiled=True)
    projected = jnp.dot(attn_in, w_qkv, preferred_element_type=jnp.float32).astype(jnp.bfloat16)
    row_major = lax.all_to_all(projected, "tp", split_axis=0, concat_axis=1, tiled=True)
    attended = attend(row_major, kv_cache, positions)
    head_major = lax.all_to_all(attended, "tp", split_axis=1, concat_axis=0, tiled=True)
    picked = head_major
    attn_sum = lax.psum_scatter(
        jnp.dot(picked, w_out, preferred_element_type=jnp.float32),
        "tp",
        scatter_dimension=0,
        tiled=True,
    )
    middle = (stream_in.astype(jnp.float32) + attn_sum).astype(jnp.bfloat16)
    own_ffn = rms_norm(middle.astype(jnp.float32), norm_gains[1]).astype(jnp.bfloat16)
    ffn_in = lax.all_gather(own_ffn, "tp", axis=0, tiled=True)
    grouped = ffn_in.astype(jnp.float32).reshape(mem_dev, batch_rows, width)
    gate_in = (grouped * fast_in[:, 0][:, None, :]).astype(jnp.bfloat16).reshape(all_rows, width)
    up_in = (grouped * fast_in[:, 1][:, None, :]).astype(jnp.bfloat16).reshape(all_rows, width)
    hidden_cols = w_gate_up.shape[2]
    gate_act = (
        jnp.dot(gate_in, w_gate_up[0], preferred_element_type=jnp.float32).reshape(
            mem_dev, batch_rows, hidden_cols
        )
        * fast_hidden[:, 0][:, None, :]
    )
    up_act = (
        jnp.dot(up_in, w_gate_up[1], preferred_element_type=jnp.float32).reshape(
            mem_dev, batch_rows, hidden_cols
        )
        * fast_hidden[:, 1][:, None, :]
    )
    hidden = (
        (jax.nn.silu(gate_act) * up_act * fast_hidden[:, 2][:, None, :])
        .astype(jnp.bfloat16)
        .reshape(all_rows, hidden_cols)
    )
    picked = hidden
    down_sum = lax.psum_scatter(
        jnp.dot(picked, w_down, preferred_element_type=jnp.float32),
        "tp",
        scatter_dimension=0,
        tiled=True,
    )
    layer_out = (middle.astype(jnp.float32) + down_sum * own_scale).astype(jnp.bfloat16)
    own_final = rms_norm(layer_out.astype(jnp.float32), norm_gains[2]).astype(jnp.bfloat16)
    final_in = lax.all_gather(own_final, "tp", axis=0, tiled=True)
    logits = jnp.dot(final_in, lm_head, preferred_element_type=jnp.float32)
    vocab_cols = lm_head.shape[1]
    member_total = jnp.sum(logits.reshape(mem_dev, batch_rows, vocab_cols), axis=0)
    member_count = mem_dev * lax.axis_size("member")
    mean_logit = (
        lax.psum(member_total.astype(jnp.bfloat16), "member").astype(jnp.float32) / member_count
    )
    column_ids = tp_rank * vocab_cols + jnp.arange(vocab_cols)
    target_part = jnp.sum(
        jnp.where(column_ids[None, :] == targets[:, None], mean_logit, 0.0), axis=-1
    )
    local_peak = jnp.max(mean_logit, axis=-1)
    peak = lax.pmax(local_peak, "tp")
    exp_total, target_logit = lax.psum(
        (jnp.sum(jnp.exp(mean_logit - peak[:, None]), axis=-1), target_part), "tp"
    )
    token_logprob = target_logit - (peak + jnp.log(exp_total))
    return (mean_logit.astype(jnp.bfloat16), token_logprob)


BF16 = jnp.bfloat16
F32 = jnp.float32
DMA = pltpu.SemaphoreType.DMA
QUAD = 4


def norm_rows(values_in, gain):
    return (
        values_in
        * lax.rsqrt(jnp.mean(values_in * values_in, axis=-1, keepdims=True) + 1e-05)
        * gain
    )


class Place:
    def __init__(self, lines):
        self.tp = lax.axis_index("tp")
        self.member = lax.axis_index("member")
        self.lines = lines
        self.quad = lax.rem(self.tp, QUAD)
        self.line = self.tp // QUAD
        self.quad_x = self.quad + 1 - 2 * lax.rem(self.quad, 2)
        self.quad_y = lax.rem(self.quad + 2, QUAD)
        self.quad_d = self.quad_x + self.quad_y - self.quad
        self.to_x = {"tp": self.line * QUAD + self.quad_x}
        self.to_y = {"tp": self.line * QUAD + self.quad_y}

    def line_at(self, step):
        return lax.rem(self.line + step + self.lines, self.lines)

    def to_line(self, step):
        return {"tp": self.line_at(step) * QUAD + self.quad}


def remote(src, dst, send_sem, recv_sem, device):
    copy = pltpu.make_async_remote_copy(
        src_ref=src,
        dst_ref=dst,
        send_sem=send_sem,
        recv_sem=recv_sem,
        device_id=device,
        device_id_type=pl.DeviceIdType.MESH,
    )
    copy.start()
    return copy


NT = (((1,), (1,)), ((), ()))
CHUNKS = 2


class Gather:
    def __init__(self, place, buf, rows, spans, sems):
        self.place, self.buf, self.rows, self.spans = place, buf, rows, spans
        self.sends, self.recvs = sems
        self.copies = {}

    def at(self, step, quad, start, width):
        index = self.place.line_at(step) * QUAD + quad
        rows = pl.ds(pl.multiple_of(index * self.rows, self.rows), self.rows)
        return self.buf.at[rows, pl.ds(start, width)]

    def send(self, kind, k, c, block, device):
        self.copies[kind, k, c] = remote(
            block, block, self.sends.at[kind, k, c], self.recvs.at[kind, k, c], device
        )

    def start(self):
        place = self.place
        for c, (start, width) in enumerate(self.spans):
            mine = self.at(0, place.quad, start, width)
            for k in range(1, place.lines):
                self.send(0, k, c, mine, place.to_line(k))
            self.send(1, 0, c, mine, place.to_x)
            self.send(2, 0, c, mine, place.to_y)

    def spread(self, c):
        place = self.place
        for k in range(1, place.lines):
            self.copies[0, k, c].wait_recv()
            block = self.at(-k, place.quad, *self.spans[c])
            self.send(1, k, c, block, place.to_x)
            self.send(2, k, c, block, place.to_y)

    def relay(self, c):
        place = self.place
        start, width = self.spans[c]
        half = width // 2
        for k in range(place.lines):
            self.copies[1, k, c].wait_recv()
            self.send(3, k, c, self.at(-k, place.quad_x, start, half), place.to_y)
            self.copies[2, k, c].wait_recv()
            self.send(4, k, c, self.at(-k, place.quad_y, start + half, half), place.to_x)

    def arrive(self, c):
        for k in range(self.place.lines):
            self.copies[3, k, c].wait_recv()
            self.copies[4, k, c].wait_recv()

    def run(self, compute):
        count = len(self.spans)
        self.start()
        self.spread(0)
        for c in range(count):
            if c + 1 < count:
                self.spread(c + 1)
            self.relay(c)
            if c:
                self.arrive(c - 1)
                compute(*self.spans[c - 1])
        self.arrive(count - 1)
        compute(*self.spans[count - 1])
        for copy in self.copies.values():
            copy.wait_send()


class Reduce:
    def __init__(self, place, part, total, rows, spans, sems, bufs):
        self.place, self.part, self.total = place, part, total
        self.rows, self.spans = rows, spans
        self.sends, self.recvs = sems
        self.got_dx, self.got_dy, self.put_x, self.put_y = bufs[:4]
        self.got_x, self.got_y, self.put_z, self.got_z = bufs[4:]
        self.steps = list(range(1, place.lines)) + [0]
        self.copies = {}

    def at(self, step, quad):
        index = self.place.line_at(step) * QUAD + quad
        return pl.ds(pl.multiple_of(index * self.rows, self.rows), self.rows)

    def send(self, kind, k, c, src, dst, device):
        self.copies[kind, k, c] = remote(
            src, dst, self.sends.at[kind, k, c], self.recvs.at[kind, k, c], device
        )

    def halves(self, c):
        start, width = self.spans[c]
        return pl.ds(start, width // 2), pl.ds(start + width // 2, width // 2)

    def direct(self, c):
        place, part = self.place, self.part
        low, high = self.halves(c)
        for k in self.steps:
            diag = self.at(k, place.quad_d)
            self.send(0, k, c, part.at[diag, high], self.got_dx.at[k, :, low_of(c, high)], place.to_x)
            self.send(1, k, c, part.at[diag, low], self.got_dy.at[k, :, low_of(c, low)], place.to_y)
        for k in self.steps:
            self.send(2, k, c, part.at[self.at(k, place.quad_x), high], self.got_x.at[k, :, high], place.to_x)
            self.send(3, k, c, part.at[self.at(k, place.quad_y), low], self.got_y.at[k, :, low], place.to_y)

    def follow(self, c):
        place, part = self.place, self.part
        low, high = self.halves(c)
        packed = low_of(c, low)
        for k in self.steps:
            self.copies[1, k, c].wait_recv()
            self.put_x[k, :, packed] = (
                part[self.at(k, place.quad_x), low].astype(F32)
                + self.got_dy[k, :, packed].astype(F32)
            ).astype(BF16)
            self.send(4, k, c, self.put_x.at[k, :, packed], self.got_x.at[k, :, low], place.to_x)
            self.copies[0, k, c].wait_recv()
            self.put_y[k, :, packed] = (
                part[self.at(k, place.quad_y), high].astype(F32)
                + self.got_dx[k, :, packed].astype(F32)
            ).astype(BF16)
            self.send(5, k, c, self.put_y.at[k, :, packed], self.got_y.at[k, :, high], place.to_y)

    def settle(self, c):
        place, part = self.place, self.part
        span = pl.ds(*self.spans[c])
        for k in self.steps:
            for kind in (2, 3, 4, 5):
                self.copies[kind, k, c].wait_recv()
            quad_sum = (
                part[self.at(k, place.quad), span].astype(F32)
                + self.got_x[k, :, span].astype(F32)
                + self.got_y[k, :, span].astype(F32)
            )
            if k:
                self.put_z[k, :, span] = quad_sum.astype(BF16)
                self.send(6, k, c, self.put_z.at[k, :, span], self.got_z.at[k, :, span], place.to_line(k))
            else:
                self.total[:, span] = quad_sum

    def run(self, compute):
        count = len(self.spans)
        compute(*self.spans[0])
        self.direct(0)
        for c in range(count):
            if c + 1 < count:
                compute(*self.spans[c + 1])
                self.direct(c + 1)
            self.follow(c)
            if c:
                self.settle(c - 1)
        self.settle(count - 1)
        for c in range(count):
            span = pl.ds(*self.spans[c])
            for k in self.steps[:-1]:
                self.copies[6, k, c].wait_recv()
                self.total[:, span] += self.got_z[k, :, span].astype(F32)
        for copy in self.copies.values():
            copy.wait_send()


def low_of(c, span):
    return pl.ds(c * span.size, span.size)


def attend_row(region, row, query, fresh_keys, fresh_values, position, count, key_heads):
    head_size = query.shape[1]
    group = query.shape[0] // key_heads
    kv_cols = key_heads * head_size
    inv_root = head_size ** (-0.5)
    wide = jnp.concatenate([query] * key_heads, axis=1)
    owner = lax.broadcasted_iota(jnp.int32, wide.shape, 0) // group
    column = lax.broadcasted_iota(jnp.int32, wide.shape, 1) // head_size
    wide = jnp.where(owner == column, wide, 0.0).astype(BF16)
    span = pl.ds(pl.multiple_of(row * count, count), count)
    scores = lax.dot_general(wide, region[span, :kv_cols], NT, preferred_element_type=F32) * inv_root
    fresh = lax.dot_general(wide, fresh_keys, NT, preferred_element_type=F32) * inv_root
    spot = lax.broadcasted_iota(jnp.int32, scores.shape, 1).astype(F32)
    scores = jnp.where(spot < position, scores, -1e30)
    fresh = jnp.where(lax.broadcasted_iota(jnp.int32, fresh.shape, 1) == row, fresh, -1e30)
    peak = jnp.maximum(
        jnp.max(scores, axis=1, keepdims=True), jnp.max(fresh, axis=1, keepdims=True)
    )
    weights = jnp.exp(scores - peak)
    fresh_w = jnp.exp(fresh - peak)
    scale = 1.0 / (
        jnp.sum(weights, axis=1, keepdims=True) + jnp.sum(fresh_w, axis=1, keepdims=True)
    )
    full = jnp.dot(
        (weights * scale).astype(BF16), region[span, kv_cols:], preferred_element_type=F32
    ) + jnp.dot((fresh_w * scale).astype(BF16), fresh_values, preferred_element_type=F32)
    full = jnp.where(owner == column, full, 0.0)
    result = full[:, :head_size]
    for k in range(1, key_heads):
        result = result + full[:, k * head_size : (k + 1) * head_size]
    return result


def layer_kernel(
    lines, names, stream, cache, w_qkv, w_out, w_gate_up, w_down, lm_head,
    table, factors, inner, targets, out, logprob, *refs
):
    s = SimpleNamespace(**dict(zip(names, refs)))
    place = Place(lines)
    tp_count = lines * QUAD
    member = place.member
    other = {"member": 1 - member}
    own_rows, width = s.own.shape
    region, gate_up, block = s.region, s.gate_up, s.block
    count = cache.shape[1]
    ff = w_down.shape[0]
    half = width // 2

    loads = {}

    def load(name, i, src, dst):
        loads[name] = pltpu.make_async_copy(src, dst, s.loads.at[i])
        loads[name].start()

    barrier = pltpu.get_barrier_semaphore()
    others = []
    for core in (member, 1 - member):
        for step in range(tp_count):
            if others or step:
                others.append({"member": core, "tp": lax.rem(place.tp + step, tp_count)})
    for device in others:
        pl.semaphore_signal(barrier, inc=1, device_id=device, device_id_type=pl.DeviceIdType.MESH)
    load("stream", 0, stream, s.stream)
    qkv = gate_up.at[0, :, pl.ds(0, w_qkv.shape[1])]
    load("qkv", 1, w_qkv, qkv)
    for r in range(own_rows):
        load(("row", r), 6 + r, cache.at[r], region.at[pl.ds(r * count, count)])
    load("out", 2, w_out, s.w_out)
    loads["stream"].wait()
    mine = pl.ds(pl.multiple_of(place.tp * own_rows, own_rows), own_rows)
    block[mine, :] = norm_rows(s.stream[...].astype(F32), factors[0:1, :]).astype(BF16)
    pl.semaphore_wait(barrier, len(others))

    piece = width // CHUNKS
    spans = [(c * piece, piece) for c in range(CHUNKS)]
    first_sums = s.acts.at[0, :, pl.ds(0, w_qkv.shape[1])]
    waited = []

    def project(start, size):
        if not waited:
            loads["qkv"].wait()
            waited.append(True)
        span = pl.ds(start, size)
        step = jnp.dot(block[:, span], qkv[span, :], preferred_element_type=F32)
        if start:
            first_sums[...] += step
        else:
            first_sums[...] = step

    Gather(place, block, own_rows, spans, (s.ga_send, s.ga_recv)).run(project)
    s.proj[...] = first_sums[...].astype(BF16)
    load("gate_up", 3, w_gate_up, gate_up)

    def peers(k):
        return lax.rem(place.tp + k, tp_count)

    copies = []
    for k in range(1, tp_count):
        rows = pl.ds(pl.multiple_of(peers(k) * own_rows, own_rows), own_rows)
        copies.append(
            remote(
                s.proj.at[rows], s.rows_in.at[place.tp],
                s.xa_send.at[k], s.xa_recv.at[k], {"tp": peers(k)},
            )
        )
    s.rows_in[place.tp] = s.proj[mine, :]
    for copy in copies:
        copy.wait_recv()
    per_device = s.proj.shape[1] // HD
    cos, sin = table[0], table[1]

    def head(h):
        column = (h % per_device) * HD
        return s.rows_in[h // per_device, :, column : column + HD]

    def turned(h):
        value = head(h).astype(F32)
        return (value * cos + pltpu.roll(value, HD // 2, 1) * sin).astype(BF16)

    for h in range(HEADS):
        s.queries[h * own_rows : (h + 1) * own_rows, :] = turned(h).astype(F32)
    for k in range(KV):
        s.keys[:, k * HD : (k + 1) * HD] = turned(HEADS + k)
        s.values[:, k * HD : (k + 1) * HD] = head(HEADS + KV + k)
    for r in range(own_rows):
        loads["row", r].wait()
    unroll = 4

    @pl.loop(0, own_rows // unroll)
    def _(i):
        for j in range(unroll):
            r = i * unroll + j
            strided = pl.ds(r, HEADS, stride=own_rows)
            s.attended[strided, :] = attend_row(
                region, r, s.queries[strided, :], s.keys[...], s.values[...],
                table[2, pl.ds(r, 1), :][:, :1], count, KV,
            )

    load("down_0", 4, w_down.at[:, pl.ds(0, half)], region.at[pl.ds(width, ff)])
    load("down_1", 5, w_down.at[:, pl.ds(half, half)], region.at[pl.ds(width + ff, ff)])
    cols = lm_head.shape[1] // 2
    load(
        "words", 0, lm_head.at[:, pl.ds(pl.multiple_of(member * cols, cols), cols)],
        region.at[pl.ds(0, width)],
    )
    own_heads = w_out.shape[0] // HD
    for d in range(tp_count):
        for i in range(own_heads):
            h = d * own_heads + i
            s.heads_out[d, :, i * HD : (i + 1) * HD] = s.attended[
                h * own_rows : (h + 1) * own_rows, :
            ].astype(BF16)
    for copy in copies:
        copy.wait_send()
    copies = []
    for k in range(1, tp_count):
        copies.append(
            remote(
                s.heads_out.at[peers(k)], s.heads_in.at[mine],
                s.xb_send.at[k], s.xb_recv.at[k], {"tp": peers(k)},
            )
        )
    s.heads_in[mine, :] = s.heads_out[place.tp]
    loads["out"].wait()
    for copy in copies:
        copy.wait_recv()
    part, total = s.part, s.total
    sums = [s.got_dx, s.got_dy, s.put_x, s.put_y, s.got_x, s.got_y, s.put_z, s.got_z]

    def project_out(start, size):
        span = pl.ds(start, size)
        part[:, span] = jnp.dot(
            s.heads_in[...], s.w_out[:, span], preferred_element_type=F32
        ).astype(BF16)

    Reduce(place, part, total, own_rows, spans, (s.ra_send, s.ra_recv), sums).run(project_out)
    for copy in copies:
        copy.wait_send()
    middle = s.middle
    middle[...] = (s.stream[...].astype(F32) + total[...]).astype(BF16)
    block[mine, :] = norm_rows(middle[...].astype(F32), factors[1:2, :]).astype(BF16)
    members, batch = 2, s.final.shape[1]
    acts, hidden = s.acts, s.hidden
    waited_up = []

    def gate_and_up(start, size):
        if not waited_up:
            loads["gate_up"].wait()
            acts[...] = jnp.zeros_like(acts)
            waited_up.append(True)
        wide = 512

        @pl.loop(0, size // wide)
        def _(i):
            span = pl.ds(pl.multiple_of(start + i * wide, wide), wide)
            values = block[:, span].astype(F32)
            for j in range(2):
                scaled = jnp.concatenate(
                    [
                        values[m * batch : (m + 1) * batch] * factors[3 + 2 * m + j : 4 + 2 * m + j, span]
                        for m in range(members)
                    ],
                    axis=0,
                ).astype(BF16)
                acts[j] += jnp.dot(scaled, gate_up[j, span, :], preferred_element_type=F32)

    Gather(place, block, own_rows, spans, (s.gb_send, s.gb_recv)).run(gate_and_up)
    for m in range(members):
        rows = slice(m * batch, (m + 1) * batch)
        gate = acts[0, rows, :] * inner[3 * m : 3 * m + 1, :]
        hidden[rows, :] = (
            gate / (1.0 + jnp.exp(-gate))
            * (acts[1, rows, :] * inner[3 * m + 1 : 3 * m + 2, :])
            * inner[3 * m + 2 : 3 * m + 3, :]
        ).astype(BF16)
    loads["down_0"].wait()
    loads["down_1"].wait()

    def project_down(start, size):
        side = start // half
        rows = pl.ds(width + side * ff, ff)
        part[:, pl.ds(start, size)] = jnp.dot(
            hidden[...], region[rows, pl.ds(start - side * half, size)],
            preferred_element_type=F32,
        ).astype(BF16)

    Reduce(place, part, total, own_rows, spans, (s.rb_send, s.rb_recv), sums).run(project_down)
    own_member = place.tp * own_rows // batch
    scale = jnp.where(own_member == 0, factors[7:8, :], factors[8:9, :])
    layer_out = (middle[...].astype(F32) + total[...] * scale).astype(BF16)
    s.own[...] = norm_rows(layer_out.astype(F32), factors[2:3, :]).astype(BF16)
    first = member == 0
    low, high = s.own[:, :half].astype(F32), s.own[:, half:].astype(F32)
    half_own, pair = s.half_own, s.pair
    half_own[...] = jnp.where(first, low, high)
    s.away[...] = jnp.where(first, high, low).astype(BF16)
    core = remote(s.away, s.from_core, s.side_send.at[0], s.side_recv.at[0], other)
    core.wait_recv()
    half_own[...] = half_own[...] + s.from_core[...].astype(F32)
    pair[...] = half_own[...]
    twin = remote(
        pair, s.from_pair, s.side_send.at[1], s.side_recv.at[1], place.to_line(lines // 2)
    )
    twin.wait_recv()
    turn = 1 - 2 * lax.rem(place.line, 2)

    class Pairwise:
        lines = 2
        quad, quad_x, quad_y = place.quad, place.quad_x, place.quad_y
        to_x, to_y = place.to_x, place.to_y

        @staticmethod
        def line_at(step):
            return lax.rem(place.line + abs(step), 2)

        @staticmethod
        def to_line(step):
            return {"tp": (place.line + turn) * QUAD + place.quad}

    final = s.final
    at = lax.rem(place.line, 2) * QUAD + place.quad
    final[member, pl.ds(pl.multiple_of(at * own_rows, own_rows), own_rows), :] = (
        (half_own[...] + s.from_pair[...]) * 0.25
    ).astype(BF16)
    words = region.at[pl.ds(0, width)]
    shares = []

    def share(start, size):
        view = final.at[member, :, pl.ds(start, size)]
        shares.append(
            remote(
                view, view, s.share_send.at[len(shares)], s.share_recv.at[len(shares)], other
            )
        )

    last = half // 2
    Gather(
        Pairwise, final.at[member], own_rows, [(0, last), (last, last)], (s.gc_send, s.gc_recv)
    ).run(share)
    loads["words"].wait()
    for copy in shares:
        copy.wait_recv()
    tile_count = s.tile_send.shape[0]
    tile_width = cols // tile_count
    column = lax.broadcasted_iota(jnp.int32, (batch, batch), 1)
    corner = lax.broadcasted_iota(jnp.int32, (batch, batch), 0) == column
    wanted = jnp.sum(
        jnp.where(corner, targets[...].astype(F32), 0.0), axis=-1, keepdims=True
    ).astype(jnp.int32)
    peak = jnp.full((batch, 1), -jnp.inf, F32)
    amount = jnp.zeros((batch, 1), F32)
    found = jnp.zeros((batch, 1), F32)
    tiles = []
    for i in range(tile_count):
        span = pl.ds(i * tile_width, tile_width)
        tile = jnp.dot(final[0], words[:half, span], preferred_element_type=F32) + jnp.dot(
            final[1], words[half:, span], preferred_element_type=F32
        )
        into = out.at[:, pl.ds(pl.multiple_of(member * cols + i * tile_width, tile_width), tile_width)]
        into[...] = tile.astype(BF16)
        tiles.append(remote(into, into, s.tile_send.at[i], s.tile_recv.at[i], other))
        new = jnp.maximum(peak, jnp.max(tile, axis=-1, keepdims=True))
        amount = amount * jnp.exp(peak - new) + jnp.sum(
            jnp.exp(tile - new), axis=-1, keepdims=True
        )
        peak = new
        column = (
            (place.tp * 2 + member) * cols
            + i * tile_width
            + lax.broadcasted_iota(jnp.int32, tile.shape, 1)
        )
        found = found + jnp.sum(jnp.where(column == wanted, tile, 0.0), axis=-1, keepdims=True)
    lane = lax.broadcasted_iota(jnp.int32, (batch, 128), 1)
    facts = jnp.where(lane == 0, peak, jnp.where(lane == 1, amount, found))
    stats, board = s.stats, s.board
    stats[...] = jnp.transpose(facts)[:8, :]
    copies = []
    for slot, device in enumerate(others):
        copies.append(
            remote(
                stats, board.at[slot + 1], s.stat_send.at[slot], s.stat_recv.at[slot], device
            )
        )
    board[0] = stats[...]
    for copy in copies:
        copy.wait_recv()
    top = jnp.max(board[:, 0, :], axis=0, keepdims=True)
    amount = jnp.sum(board[:, 1, :] * jnp.exp(board[:, 0, :] - top), axis=0, keepdims=True)
    found = jnp.sum(board[:, 2, :], axis=0, keepdims=True)
    logprob[...] = found - (top + jnp.log(amount))
    for copy in tiles:
        copy.wait_recv()
    for copy in [core, twin] + shares + tiles + copies:
        copy.wait_send()


VMEM = pl.BlockSpec(memory_space=pltpu.VMEM)
ANY = pl.BlockSpec(memory_space=pl.ANY)


def fused_body(
    stream_in,
    kv_cache,
    lengths,
    targets,
    norm_gains,
    w_qkv,
    w_out,
    w_gate_up,
    w_down,
    lm_head,
    fast_in,
    fast_hidden,
    fast_out,
):
    tp_count = lax.axis_size("tp")
    tp_rank = lax.axis_index("tp")
    lines = tp_count // QUAD
    batch = lengths.shape[0]
    own_rows, width = stream_in.shape
    all_rows = own_rows * tp_count
    half = width // 2
    devices = 2 * tp_count
    vocab_cols = lm_head.shape[1]
    ff = w_down.shape[0]
    positions = lax.dynamic_slice_in_dim(
        lengths, (tp_rank * own_rows) % batch, own_rows, 0
    ).astype(F32)
    frequency = ROPE_BASE ** (-jnp.arange(HD // 2, dtype=F32) * 2.0 / HD)
    angles = positions[:, None] * frequency[None, :]
    cos, sin = jnp.cos(angles), jnp.sin(angles)
    table = jnp.stack(
        [
            jnp.concatenate([cos, cos], axis=1),
            jnp.concatenate([-sin, sin], axis=1),
            jnp.broadcast_to(positions[:, None], (own_rows, HD)),
        ]
    )
    factors = jnp.concatenate(
        [norm_gains, fast_in.reshape(4, width), fast_out, jnp.zeros((7, width), F32)]
    )
    inner = jnp.concatenate([fast_hidden.reshape(6, ff), jnp.zeros((10, ff), F32)])
    tiles = 4
    small = pltpu.VMEM((lines, own_rows, half), BF16)
    large = pltpu.VMEM((lines, own_rows, width), BF16)
    own = pltpu.VMEM((own_rows, width), BF16)
    gather = DMA((5, lines, CHUNKS))
    reduce = DMA((7, lines, CHUNKS))
    scratch = dict(
        region=pltpu.VMEM((own_rows * kv_cache.shape[1], kv_cache.shape[2]), BF16),
        gate_up=pltpu.VMEM(w_gate_up.shape, BF16),
        w_out=pltpu.VMEM(w_out.shape, BF16),
        block=pltpu.VMEM((all_rows, width), BF16),
        part=pltpu.VMEM((all_rows, width), BF16),
        stream=own,
        own=own,
        middle=own,
        total=pltpu.VMEM((own_rows, width), F32),
        proj=pltpu.VMEM((all_rows, w_qkv.shape[1]), BF16),
        rows_in=pltpu.VMEM((tp_count, own_rows, w_qkv.shape[1]), BF16),
        queries=pltpu.VMEM(((HEADS + 1) * own_rows, HD), F32),
        keys=pltpu.VMEM((own_rows, KV * HD), BF16),
        values=pltpu.VMEM((own_rows, KV * HD), BF16),
        attended=pltpu.VMEM(((HEADS + 1) * own_rows, HD), F32),
        heads_out=pltpu.VMEM((tp_count, own_rows, w_out.shape[0]), BF16),
        heads_in=pltpu.VMEM((all_rows, w_out.shape[0]), BF16),
        acts=pltpu.VMEM((2, all_rows, ff), F32),
        hidden=pltpu.VMEM((all_rows, ff), BF16),
        half_own=pltpu.VMEM((own_rows, half), F32),
        away=pltpu.VMEM((own_rows, half), BF16),
        from_core=pltpu.VMEM((own_rows, half), BF16),
        pair=pltpu.VMEM((own_rows, half), F32),
        from_pair=pltpu.VMEM((own_rows, half), F32),
        final=pltpu.VMEM((2, batch, half), BF16),
        stats=pltpu.VMEM((8, batch), F32),
        board=pltpu.VMEM((devices, 8, batch), F32),
        got_dx=small, got_dy=small, put_x=small, put_y=small,
        got_x=large, got_y=large, put_z=large, got_z=large,
        loads=DMA((6 + own_rows,)),
        ga_send=gather, ga_recv=gather, gb_send=gather, gb_recv=gather,
        ra_send=reduce, ra_recv=reduce, rb_send=reduce, rb_recv=reduce,
        gc_send=DMA((5, 2, 2)), gc_recv=DMA((5, 2, 2)),
        xa_send=DMA((tp_count,)), xa_recv=DMA((tp_count,)),
        xb_send=DMA((tp_count,)), xb_recv=DMA((tp_count,)),
        side_send=DMA((2,)), side_recv=DMA((2,)),
        share_send=DMA((2,)), share_recv=DMA((2,)),
        tile_send=DMA((tiles,)), tile_recv=DMA((tiles,)),
        stat_send=DMA((devices,)), stat_recv=DMA((devices,)),
    )
    mean_logits, logprob = pl.pallas_call(
        functools.partial(layer_kernel, lines, tuple(scratch)),
        out_shape=[
            jax.ShapeDtypeStruct((batch, vocab_cols), BF16),
            jax.ShapeDtypeStruct((1, batch), F32),
        ],
        in_specs=[ANY] * 7 + [VMEM] * 4,
        out_specs=[VMEM, VMEM],
        scratch_shapes=list(scratch.values()),
        compiler_params=pltpu.CompilerParams(
            collective_id=1, has_side_effects=True, vmem_limit_bytes=VMEM_BYTES
        ),
    )(
        stream_in, kv_cache, w_qkv, w_out, w_gate_up, w_down, lm_head,
        table, factors, inner, targets[None, :],
    )
    return (mean_logits, logprob[0])


VMEM_BYTES = 67043328


def body(*args):
    stream_in, kv_cache, lengths = args[0], args[1], args[2]
    w_qkv, w_out, w_down, lm_head, fast_in = args[5], args[6], args[8], args[9], args[10]
    own_rows, width = stream_in.shape
    batch, ff = lengths.shape[0], w_down.shape[0]
    tp_count = lax.axis_size("tp")
    fits = (
        tp_count == 4 * QUAD
        and own_rows == 16
        and batch == 128
        and lax.axis_size("member") == 2
        and fast_in.shape[0] == 2
        and own_rows * tp_count == 2 * batch
        and w_qkv.shape[1] % HD == 0
        and w_out.shape[0] % HD == 0
        and w_qkv.shape[1] <= ff
        and width % (256 * CHUNKS) == 0
        and kv_cache.shape[2] * 2 == width
        and lm_head.shape[1] == width
        and own_rows * kv_cache.shape[1] >= width + 2 * ff
    )
    if fits:
        return fused_body(*args)
    return plain_body(*args)


def solution(mesh):
    in_specs = (
        P(("member", "tp"), None),
        P(("member", "tp"), None, None),
        P(),
        P(),
        P(),
        P(None, "tp"),
        P("tp", None),
        P(None, None, "tp"),
        P("tp", None),
        P(None, "tp"),
        P("member", None, None),
        P("member", None, "tp"),
        P("member", None),
    )
    out_specs = (P(None, "tp"), P())
    return jax.shard_map(body, mesh=mesh, in_specs=in_specs, out_specs=out_specs, check_vma=False)
```

time: 209 us -> 170 us (0.81)
  waiting for transfers between devices: 14.2 us -> 0 us
  starting transfers between devices: 10.6 us -> 0 us
  Pallas kernels: 170 us -> 160 us
  local copies, waits for them, and re-layouts: 10 us -> 5.84 us
  other arithmetic: 0.67 us -> 3.2 us
    all_to_all x2 -> x0, waiting for transfers between devices: 14.2 us -> none  [the longest x1 7.13 us: linked_body(): lax.all_to_all(attended, 'tp', split_axis=1, concat_axis=0, tiled=True)]
    all_to_all x2 -> x0, starting transfers between devices: 10.6 us -> none  [the longest x1 7.07 us: linked_body(): lax.all_to_all(projected, 'tp', split_axis=0, concat_axis=1, tiled=True)]
    pallas_call x3 -> x1, Pallas kernels: 170 us -> 160 us  [fused_body(): pl.pallas_call(functools.partial(layer_kernel, lines, tuple(scratch)), ou...]
    broadcast_in_dim x6 -> x1, local copies, waits for them, and re-layouts: 3.11 us -> 0.01 us  [fused_body(): jnp.zeros((7, width), F32)]
    unnamed x26 -> x3, local copies, waits for them, and re-layouts: 4.5 us -> 4.15 us
  transfers between devices with their start and end apart: 2 -> 0, of which waited for: 2 -> 0; matrix products, arithmetic and copies ran while one was open for 1% -> 0% of each run, Pallas kernels for 0% -> 0%
where the time goes in v1:
time: 170 us
  Pallas kernels  160 us (94%)
  local copies, waits for them, and re-layouts  5.84 us (3%)
  other arithmetic  3.2 us (2%)
    pallas_call x1, Pallas kernels, fused_body(): pl.pallas_call(functools.partial(layer_kernel, lines, tuple(scratch)), ou...  160 us
    unnamed x3, local copies, waits for them, and re-layouts  4.15 us

profile of v1, /device:TPU:0, one launch (start us, length us, event | category | flops | bytes accessed | tf_op | source)
XLA Modules:
  0.0 169.8 jit_solution(2601032325612300790)
XLA Ops:
  0.6 0.7 dynamic-slice_convert_fusion
  1.4 0.1 pad.4.clone
  1.5 0.1 stack_broadcast_in_dim.2
  1.5 0.1 multiply_cosine_fusion
  1.7 0.1 maximum_bitcast_fusion
  1.7 0.6 pad_maximum_fusion.table
  2.4 0.7 copy.16
  3.1 0.6 concatenate.15.inner
  3.7 0.9 reshape.17
  4.6 1.7 maximum_maximum_fusion.factors
  6.3 160.1 %shard_map.140 = (bf16[128,4096]{1,0:T(8,128)(2,1)}, f32[1,128]{1,0:T(1,128)}) custom-call(bf16[16,4096]{1,0:T(8,128)(2,1)} %stream.1, bf16[16,512,2048]{2,1,0:T(8,128)(2,1)} %cache.1, bf16[4096,384]{1,0:T(8,128)(2,1)} %w_qkv.1, bf16[256,4096]{1,0:T(8,128)(2,1)} %w_out.1, bf16[2,4096,896]{2,1,0:T(8,128)(2,1)} %w_gate_up.1, bf16[896,4096]{1,0:T(8,128)(2,1)} %w_down.1, ...), custom_call_target="tpu_custom_call" | custom-call | tf_op jit(solution)/shard_map/pallas_call | solution.py:816
  166.4 2.3 %copy.19 = bf16[128,4096]{1,0:T(8,128)(2,1)} copy(bf16[128,4096]{1,0:T(8,128)(2,1)} %get-tuple-element.13) | data formatting | bytes 2097152
  168.7 1.1 copy.20
  (3 shorter events, 0.0 us)

commit v2 on v1

--- a/solution.py
+++ b/solution.py
@@ -200,6 +200,20 @@
         self.quad_d = self.quad_x + self.quad_y - self.quad
         self.to_x = {"tp": self.line * QUAD + self.quad_x}
         self.to_y = {"tp": self.line * QUAD + self.quad_y}
+        self.inner = jnp.logical_or(self.line == 1, self.line == 2)
+        beside, across, over = (
+            self.line + 1 - 2 * lax.rem(self.line, 2),
+            lines - 1 - self.line,
+            lax.rem(self.line + 2, lines),
+        )
+        self.near = [
+            self.line,
+            beside,
+            jnp.where(self.inner, across, over),
+            jnp.where(self.inner, over, across),
+        ]
+        self.pair = {"tp": beside * QUAD + self.quad}
+        self.middle = {"tp": across * QUAD + self.quad}
 
     def line_at(self, step):
         return lax.rem(self.line + step + self.lines, self.lines)
@@ -223,9 +237,10 @@
 
 NT = (((1,), (1,)), ((), ()))
 CHUNKS = 2
-
-
-class Gather:
+WORD_LOADS = 8
+
+
+class PairGather:
     def __init__(self, place, buf, rows, spans, sems):
         self.place, self.buf, self.rows, self.spans = place, buf, rows, spans
         self.sends, self.recvs = sems
@@ -257,6 +272,7 @@
             block = self.at(-k, place.quad, *self.spans[c])
             self.send(1, k, c, block, place.to_x)
             self.send(2, k, c, block, place.to_y)
+            self.feed()
 
     def relay(self, c):
         place = self.place
@@ -267,14 +283,16 @@
             self.send(3, k, c, self.at(-k, place.quad_x, start, half), place.to_y)
             self.copies[2, k, c].wait_recv()
             self.send(4, k, c, self.at(-k, place.quad_y, start + half, half), place.to_x)
+            self.feed()
 
     def arrive(self, c):
         for k in range(self.place.lines):
             self.copies[3, k, c].wait_recv()
             self.copies[4, k, c].wait_recv()
 
-    def run(self, compute):
+    def run(self, compute, feed=lambda: None):
         count = len(self.spans)
+        self.feed = feed
         self.start()
         self.spread(0)
         for c in range(count):
@@ -288,6 +306,146 @@
         compute(*self.spans[count - 1])
         for copy in self.copies.values():
             copy.wait_send()
+
+
+class Gather:
+    def __init__(self, place, buf, rows, spans, side, sems):
+        self.place, self.buf, self.rows = place, buf, rows
+        self.spans, self.side = spans, side
+        self.sends, self.recvs = sems
+        self.copies, self.guarded = {}, []
+
+    def at(self, line, quad, start, width):
+        index = line * QUAD + quad
+        rows = pl.ds(pl.multiple_of(index * self.rows, self.rows), self.rows)
+        return self.buf.at[rows, pl.ds(start, width)]
+
+    def plane(self, line, start, width):
+        rows = QUAD * self.rows
+        return self.buf.at[pl.ds(pl.multiple_of(line * rows, rows), rows), pl.ds(start, width)]
+
+    def send(self, kind, k, c, block, device):
+        self.copies[kind, k, c] = remote(
+            block, block, self.sends.at[kind, k, c], self.recvs.at[kind, k, c], device
+        )
+
+    def cross(self, slot, k, c, block, device, inner):
+        copy = pltpu.make_async_remote_copy(
+            src_ref=block, dst_ref=block,
+            send_sem=self.sends.at[slot, k, c], recv_sem=self.recvs.at[0, slot_of(slot, k), c],
+            device_id=device, device_id_type=pl.DeviceIdType.MESH,
+        )
+        if inner:
+            self.guarded.append(copy)
+
+            @pl.when(self.place.inner)
+            def _():
+                copy.start()
+        else:
+            copy.start()
+            self.copies[slot, k, c] = copy
+
+    def await_line(self, k, c, block):
+        pltpu.make_async_remote_copy(
+            src_ref=block, dst_ref=block,
+            send_sem=self.sends.at[0, k, c], recv_sem=self.recvs.at[0, k, c],
+            device_id=self.place.pair, device_id_type=pl.DeviceIdType.MESH,
+        ).wait_recv()
+
+    def own_line(self, c, block):
+        self.cross(5, 0, c, block, self.place.pair, False)
+        self.cross(6, 0, c, block, self.place.middle, True)
+
+    def pass_line(self, k, c, block):
+        if k == 1:
+            self.cross(6, 1, c, block, self.place.middle, True)
+        else:
+            self.cross(5, k - 1, c, block, self.place.pair, True)
+
+    def start(self):
+        place = self.place
+        count = len(self.spans)
+        for c, span in enumerate(self.spans):
+            self.own_line(c, self.at(place.line, place.quad, *span))
+        for c, span in [(count, self.side)] + list(enumerate(self.spans)):
+            mine = self.at(place.line, place.quad, *span)
+            self.send(1, 0, c, mine, place.to_x)
+            self.send(2, 0, c, mine, place.to_y)
+
+    def spread(self, c):
+        place = self.place
+        for k in range(1, place.lines):
+            block = self.at(place.near[k], place.quad, *self.spans[c])
+            self.await_line(k, c, block)
+            self.pass_line(k, c, block)
+            self.send(1, k, c, block, place.to_x)
+            self.send(2, k, c, block, place.to_y)
+            self.feed()
+
+    def relay(self, c, k):
+        place = self.place
+        start, width = (self.spans + [self.side])[c]
+        half = width // 256 * 128
+        self.copies[1, k, c].wait_recv()
+        self.send(3, k, c, self.at(place.near[k], place.quad_x, start, half), place.to_y)
+        self.copies[2, k, c].wait_recv()
+        self.send(
+            4, k, c, self.at(place.near[k], place.quad_y, start + half, width - half), place.to_x
+        )
+
+    def arrive(self, c):
+        for k in range(self.place.lines):
+            self.copies[3, k, c].wait_recv()
+            self.copies[4, k, c].wait_recv()
+
+    def side_step(self, k):
+        c = len(self.spans)
+        if k == 0:
+            self.copies[3, 0, c].wait_recv()
+            self.copies[4, 0, c].wait_recv()
+            self.own_line(c, self.plane(self.place.line, *self.side))
+        else:
+            block = self.plane(self.place.near[k], *self.side)
+            self.await_line(k, c, block)
+            self.pass_line(k, c, block)
+
+    def run(self, compute, feed=lambda: None):
+        place = self.place
+        count = len(self.spans)
+        self.feed = feed
+        self.start()
+        self.relay(count, 0)
+        self.spread(0)
+        self.side_step(0)
+        for c in range(count):
+            if c + 1 < count:
+                self.spread(c + 1)
+            if c:
+                self.side_step(c)
+            for k in range(place.lines):
+                self.relay(c, k)
+                self.feed()
+            if c:
+                self.arrive(c - 1)
+                compute(*self.spans[c - 1])
+        for k in range(count, place.lines):
+            self.side_step(k)
+        compute(*self.side)
+        self.arrive(count - 1)
+        compute(*self.spans[count - 1])
+        for copy in self.copies.values():
+            copy.wait_send()
+
+        @pl.when(place.inner)
+        def _():
+            for copy in self.guarded:
+                copy.wait_send()
+
+
+def slot_of(slot, k):
+    if slot == 5:
+        return k + 1
+    return k + 2
 
 
 class Reduce:
@@ -341,6 +499,7 @@
                 + self.got_dx[k, :, packed].astype(F32)
             ).astype(BF16)
             self.send(5, k, c, self.put_y.at[k, :, packed], self.got_y.at[k, :, high], place.to_y)
+            self.feed()
 
     def settle(self, c):
         place, part = self.place, self.part
@@ -358,9 +517,11 @@
                 self.send(6, k, c, self.put_z.at[k, :, span], self.got_z.at[k, :, span], place.to_line(k))
             else:
                 self.total[:, span] = quad_sum
-
-    def run(self, compute):
+            self.feed()
+
+    def run(self, compute, feed=lambda: None):
         count = len(self.spans)
+        self.feed = feed
         compute(*self.spans[0])
         self.direct(0)
         for c in range(count):
@@ -419,7 +580,7 @@
 
 def layer_kernel(
     lines, names, stream, cache, w_qkv, w_out, w_gate_up, w_down, lm_head,
-    table, factors, inner, targets, out, logprob, *refs
+    table, gains, fast_in, fast_hidden, fast_out, targets, out, logprob, *refs
 ):
     s = SimpleNamespace(**dict(zip(names, refs)))
     place = Place(lines)
@@ -449,16 +610,26 @@
     load("stream", 0, stream, s.stream)
     qkv = gate_up.at[0, :, pl.ds(0, w_qkv.shape[1])]
     load("qkv", 1, w_qkv, qkv)
-    for r in range(own_rows):
-        load(("row", r), 6 + r, cache.at[r], region.at[pl.ds(r * count, count)])
-    load("out", 2, w_out, s.w_out)
+    waiting = [
+        functools.partial(load, ("row", r), 6 + r, cache.at[r], region.at[pl.ds(r * count, count)])
+        for r in range(own_rows)
+    ]
+    waiting.append(functools.partial(load, "out", 2, w_out, s.w_out))
+
+    def feed():
+        if waiting:
+            waiting.pop(0)()
+
     loads["stream"].wait()
     mine = pl.ds(pl.multiple_of(place.tp * own_rows, own_rows), own_rows)
-    block[mine, :] = norm_rows(s.stream[...].astype(F32), factors[0:1, :]).astype(BF16)
+    block[mine, :] = norm_rows(s.stream[...].astype(F32), gains[...][0:1]).astype(BF16)
     pl.semaphore_wait(barrier, len(others))
 
     piece = width // CHUNKS
     spans = [(c * piece, piece) for c in range(CHUNKS)]
+    eighth, last = width // 8, width * 5 // 16
+    parts = [(0, width - eighth - last), (width - eighth - last, last)]
+    side = (width - eighth, eighth)
     first_sums = s.acts.at[0, :, pl.ds(0, w_qkv.shape[1])]
     waited = []
 
@@ -473,9 +644,10 @@
         else:
             first_sums[...] = step
 
-    Gather(place, block, own_rows, spans, (s.ga_send, s.ga_recv)).run(project)
+    Gather(place, block, own_rows, parts, side, (s.ga_send, s.ga_recv)).run(project, feed)
+    while waiting:
+        feed()
     s.proj[...] = first_sums[...].astype(BF16)
-    load("gate_up", 3, w_gate_up, gate_up)
 
     def peers(k):
         return lax.rem(place.tp + k, tp_count)
@@ -510,6 +682,7 @@
         s.values[:, k * HD : (k + 1) * HD] = head(HEADS + KV + k)
     for r in range(own_rows):
         loads["row", r].wait()
+    load("gate_up", 3, w_gate_up, gate_up)
     unroll = 4
 
     @pl.loop(0, own_rows // unroll)
@@ -522,13 +695,24 @@
                 table[2, pl.ds(r, 1), :][:, :1], count, KV,
             )
 
-    load("down_0", 4, w_down.at[:, pl.ds(0, half)], region.at[pl.ds(width, ff)])
-    load("down_1", 5, w_down.at[:, pl.ds(half, half)], region.at[pl.ds(width + ff, ff)])
     cols = lm_head.shape[1] // 2
-    load(
-        "words", 0, lm_head.at[:, pl.ds(pl.multiple_of(member * cols, cols), cols)],
-        region.at[pl.ds(0, width)],
-    )
+    strip = pl.ds(pl.multiple_of(member * cols, cols), cols)
+    piece = width // WORD_LOADS
+    waiting.append(
+        functools.partial(load, "down_0", 4, w_down.at[:, pl.ds(0, half)], region.at[pl.ds(width, ff)])
+    )
+    waiting.append(
+        functools.partial(
+            load, "down_1", 5, w_down.at[:, pl.ds(half, half)], region.at[pl.ds(width + ff, ff)]
+        )
+    )
+    for i in range(WORD_LOADS):
+        rows = pl.ds(i * piece, piece)
+        waiting.append(
+            functools.partial(
+                load, ("words", i), 6 + own_rows + i, lm_head.at[rows, strip], region.at[rows]
+            )
+        )
     own_heads = w_out.shape[0] // HD
     for d in range(tp_count):
         for i in range(own_heads):
@@ -559,12 +743,14 @@
             s.heads_in[...], s.w_out[:, span], preferred_element_type=F32
         ).astype(BF16)
 
-    Reduce(place, part, total, own_rows, spans, (s.ra_send, s.ra_recv), sums).run(project_out)
+    Reduce(place, part, total, own_rows, spans, (s.ra_send, s.ra_recv), sums).run(project_out, feed)
+    while waiting:
+        feed()
     for copy in copies:
         copy.wait_send()
     middle = s.middle
     middle[...] = (s.stream[...].astype(F32) + total[...]).astype(BF16)
-    block[mine, :] = norm_rows(middle[...].astype(F32), factors[1:2, :]).astype(BF16)
+    block[mine, :] = norm_rows(middle[...].astype(F32), gains[...][1:2]).astype(BF16)
     members, batch = 2, s.final.shape[1]
     acts, hidden = s.acts, s.hidden
     waited_up = []
@@ -574,7 +760,7 @@
             loads["gate_up"].wait()
             acts[...] = jnp.zeros_like(acts)
             waited_up.append(True)
-        wide = 512
+        wide = 256
 
         @pl.loop(0, size // wide)
         def _(i):
@@ -583,21 +769,21 @@
             for j in range(2):
                 scaled = jnp.concatenate(
                     [
-                        values[m * batch : (m + 1) * batch] * factors[3 + 2 * m + j : 4 + 2 * m + j, span]
+                        values[m * batch : (m + 1) * batch] * fast_in[m, :, span][j : j + 1]
                         for m in range(members)
                     ],
                     axis=0,
                 ).astype(BF16)
                 acts[j] += jnp.dot(scaled, gate_up[j, span, :], preferred_element_type=F32)
 
-    Gather(place, block, own_rows, spans, (s.gb_send, s.gb_recv)).run(gate_and_up)
+    Gather(place, block, own_rows, parts, side, (s.gb_send, s.gb_recv)).run(gate_and_up)
     for m in range(members):
         rows = slice(m * batch, (m + 1) * batch)
-        gate = acts[0, rows, :] * inner[3 * m : 3 * m + 1, :]
+        gate = acts[0, rows, :] * fast_hidden[m][0:1]
         hidden[rows, :] = (
             gate / (1.0 + jnp.exp(-gate))
-            * (acts[1, rows, :] * inner[3 * m + 1 : 3 * m + 2, :])
-            * inner[3 * m + 2 : 3 * m + 3, :]
+            * (acts[1, rows, :] * fast_hidden[m][1:2])
+            * fast_hidden[m][2:3]
         ).astype(BF16)
     loads["down_0"].wait()
     loads["down_1"].wait()
@@ -612,9 +798,9 @@
 
     Reduce(place, part, total, own_rows, spans, (s.rb_send, s.rb_recv), sums).run(project_down)
     own_member = place.tp * own_rows // batch
-    scale = jnp.where(own_member == 0, factors[7:8, :], factors[8:9, :])
+    scale = jnp.where(own_member == 0, fast_out[...][0:1], fast_out[...][1:2])
     layer_out = (middle[...].astype(F32) + total[...] * scale).astype(BF16)
-    s.own[...] = norm_rows(layer_out.astype(F32), factors[2:3, :]).astype(BF16)
+    s.own[...] = norm_rows(layer_out.astype(F32), gains[...][2:3]).astype(BF16)
     first = member == 0
     low, high = s.own[:, :half].astype(F32), s.own[:, half:].astype(F32)
     half_own, pair = s.half_own, s.pair
@@ -623,7 +809,7 @@
     core = remote(s.away, s.from_core, s.side_send.at[0], s.side_recv.at[0], other)
     core.wait_recv()
     half_own[...] = half_own[...] + s.from_core[...].astype(F32)
-    pair[...] = half_own[...]
+    pair[...] = half_own[...].astype(BF16)
     twin = remote(
         pair, s.from_pair, s.side_send.at[1], s.side_recv.at[1], place.to_line(lines // 2)
     )
@@ -646,7 +832,7 @@
     final = s.final
     at = lax.rem(place.line, 2) * QUAD + place.quad
     final[member, pl.ds(pl.multiple_of(at * own_rows, own_rows), own_rows), :] = (
-        (half_own[...] + s.from_pair[...]) * 0.25
+        (half_own[...] + s.from_pair[...].astype(F32)) * 0.25
     ).astype(BF16)
     words = region.at[pl.ds(0, width)]
     shares = []
@@ -660,10 +846,11 @@
         )
 
     last = half // 2
-    Gather(
+    PairGather(
         Pairwise, final.at[member], own_rows, [(0, last), (last, last)], (s.gc_send, s.gc_recv)
     ).run(share)
-    loads["words"].wait()
+    for i in range(WORD_LOADS):
+        loads["words", i].wait()
     for copy in shares:
         copy.wait_recv()
     tile_count = s.tile_send.shape[0]
@@ -762,15 +949,12 @@
             jnp.broadcast_to(positions[:, None], (own_rows, HD)),
         ]
     )
-    factors = jnp.concatenate(
-        [norm_gains, fast_in.reshape(4, width), fast_out, jnp.zeros((7, width), F32)]
-    )
-    inner = jnp.concatenate([fast_hidden.reshape(6, ff), jnp.zeros((10, ff), F32)])
     tiles = 4
     small = pltpu.VMEM((lines, own_rows, half), BF16)
     large = pltpu.VMEM((lines, own_rows, width), BF16)
     own = pltpu.VMEM((own_rows, width), BF16)
-    gather = DMA((5, lines, CHUNKS))
+    gather_out = DMA((7, lines, CHUNKS + 1))
+    gather_in = DMA((5, lines, CHUNKS + 1))
     reduce = DMA((7, lines, CHUNKS))
     scratch = dict(
         region=pltpu.VMEM((own_rows * kv_cache.shape[1], kv_cache.shape[2]), BF16),
@@ -795,15 +979,15 @@
         half_own=pltpu.VMEM((own_rows, half), F32),
         away=pltpu.VMEM((own_rows, half), BF16),
         from_core=pltpu.VMEM((own_rows, half), BF16),
-        pair=pltpu.VMEM((own_rows, half), F32),
-        from_pair=pltpu.VMEM((own_rows, half), F32),
+        pair=pltpu.VMEM((own_rows, half), BF16),
+        from_pair=pltpu.VMEM((own_rows, half), BF16),
         final=pltpu.VMEM((2, batch, half), BF16),
         stats=pltpu.VMEM((8, batch), F32),
         board=pltpu.VMEM((devices, 8, batch), F32),
         got_dx=small, got_dy=small, put_x=small, put_y=small,
         got_x=large, got_y=large, put_z=large, got_z=large,
-        loads=DMA((6 + own_rows,)),
-        ga_send=gather, ga_recv=gather, gb_send=gather, gb_recv=gather,
+        loads=DMA((6 + own_rows + WORD_LOADS,)),
+        ga_send=gather_out, ga_recv=gather_in, gb_send=gather_out, gb_recv=gather_in,
         ra_send=reduce, ra_recv=reduce, rb_send=reduce, rb_recv=reduce,
         gc_send=DMA((5, 2, 2)), gc_recv=DMA((5, 2, 2)),
         xa_send=DMA((tp_count,)), xa_recv=DMA((tp_count,)),
@@ -819,7 +1003,7 @@
             jax.ShapeDtypeStruct((batch, vocab_cols), BF16),
             jax.ShapeDtypeStruct((1, batch), F32),
         ],
-        in_specs=[ANY] * 7 + [VMEM] * 4,
+        in_specs=[ANY] * 7 + [VMEM] * 6,
         out_specs=[VMEM, VMEM],
         scratch_shapes=list(scratch.values()),
         compiler_params=pltpu.CompilerParams(
@@ -827,7 +1011,7 @@
         ),
     )(
         stream_in, kv_cache, w_qkv, w_out, w_gate_up, w_down, lm_head,
-        table, factors, inner, targets[None, :],
+        table, norm_gains, fast_in, fast_hidden, fast_out, targets[None, :],
     )
     return (mean_logits, logprob[0])
 
@@ -851,7 +1035,7 @@
         and w_qkv.shape[1] % HD == 0
         and w_out.shape[0] % HD == 0
         and w_qkv.shape[1] <= ff
-        and width % (256 * CHUNKS) == 0
+        and width % 4096 == 0
         and kv_cache.shape[2] * 2 == width
         and lm_head.shape[1] == width
         and own_rows * kv_cache.shape[1] >= width + 2 * ff

time: 170 us -> 161 us (0.947)
  Pallas kernels: 160 us -> 154 us
    pallas_call x1, Pallas kernels: 160 us -> 154 us  [fused_body(): pl.pallas_call(functools.partial(layer_kernel, lines, tuple(scratch)), ou...]
where the time goes in v2:
time: 161 us
  Pallas kernels  154 us (96%)
  local copies, waits for them, and re-layouts  4.88 us (3%)
    pallas_call x1, Pallas kernels, fused_body(): pl.pallas_call(functools.partial(layer_kernel, lines, tuple(scratch)), ou...  154 us
    unnamed x3, local copies, waits for them, and re-layouts  4.81 us

profile of v2, /device:TPU:0, one launch (start us, length us, event | category | flops | bytes accessed | tf_op | source)
XLA Modules:
  0.0 161.2 jit_solution(10011650792186022753)
XLA Ops:
  0.6 0.7 dynamic-slice_convert_fusion
  1.4 0.1 stack_broadcast_in_dim.2
  1.5 0.1 multiply_cosine_fusion
  1.6 0.1 maximum_bitcast_fusion
  1.7 0.6 pad_maximum_fusion.table
  2.3 1.3 copy.15.fast_hidden
  3.6 154.1 %shard_map.140 = (bf16[128,4096]{1,0:T(8,128)(2,1)}, f32[1,128]{1,0:T(1,128)}) custom-call(bf16[16,4096]{1,0:T(8,128)(2,1)} %stream.1, bf16[16,512,2048]{2,1,0:T(8,128)(2,1)} %cache.1, bf16[4096,384]{1,0:T(8,128)(2,1)} %w_qkv.1, bf16[256,4096]{1,0:T(8,128)(2,1)} %w_out.1, bf16[2,4096,896]{2,1,0:T(8,128)(2,1)} %w_gate_up.1, bf16[896,4096]{1,0:T(8,128)(2,1)} %w_down.1, ...), custom_call_target="tpu_custom_call" | custom-call | tf_op jit(solution)/shard_map/pallas_call | solution.py:1000
  157.7 2.3 %copy.18 = bf16[128,4096]{1,0:T(8,128)(2,1)} copy(bf16[128,4096]{1,0:T(8,128)(2,1)} %get-tuple-element.13) | data formatting | bytes 2097152
  160.0 1.2 copy.19
  (1 shorter events, 0.0 us)

commit v3 on v2

--- a/solution.py
+++ b/solution.py
@@ -471,13 +471,18 @@
         start, width = self.spans[c]
         return pl.ds(start, width // 2), pl.ds(start + width // 2, width // 2)
 
+    def packed(self, c):
+        start, width = self.spans[c]
+        return pl.ds(start // 2, width // 2)
+
     def direct(self, c):
         place, part = self.place, self.part
         low, high = self.halves(c)
+        packed = self.packed(c)
         for k in self.steps:
             diag = self.at(k, place.quad_d)
-            self.send(0, k, c, part.at[diag, high], self.got_dx.at[k, :, low_of(c, high)], place.to_x)
-            self.send(1, k, c, part.at[diag, low], self.got_dy.at[k, :, low_of(c, low)], place.to_y)
+            self.send(0, k, c, part.at[diag, high], self.got_dx.at[k, :, packed], place.to_x)
+            self.send(1, k, c, part.at[diag, low], self.got_dy.at[k, :, packed], place.to_y)
         for k in self.steps:
             self.send(2, k, c, part.at[self.at(k, place.quad_x), high], self.got_x.at[k, :, high], place.to_x)
             self.send(3, k, c, part.at[self.at(k, place.quad_y), low], self.got_y.at[k, :, low], place.to_y)
@@ -485,7 +490,7 @@
     def follow(self, c):
         place, part = self.place, self.part
         low, high = self.halves(c)
-        packed = low_of(c, low)
+        packed = self.packed(c)
         for k in self.steps:
             self.copies[1, k, c].wait_recv()
             self.put_x[k, :, packed] = (
@@ -527,11 +532,10 @@
         for c in range(count):
             if c + 1 < count:
                 compute(*self.spans[c + 1])
+            self.follow(c)
+            if c + 1 < count:
                 self.direct(c + 1)
-            self.follow(c)
-            if c:
-                self.settle(c - 1)
-        self.settle(count - 1)
+            self.settle(c)
         for c in range(count):
             span = pl.ds(*self.spans[c])
             for k in self.steps[:-1]:
@@ -539,10 +543,6 @@
                 self.total[:, span] += self.got_z[k, :, span].astype(F32)
         for copy in self.copies.values():
             copy.wait_send()
-
-
-def low_of(c, span):
-    return pl.ds(c * span.size, span.size)
 
 
 def attend_row(region, row, query, fresh_keys, fresh_values, position, count, key_heads):
@@ -625,8 +625,8 @@
     block[mine, :] = norm_rows(s.stream[...].astype(F32), gains[...][0:1]).astype(BF16)
     pl.semaphore_wait(barrier, len(others))
 
-    piece = width // CHUNKS
-    spans = [(c * piece, piece) for c in range(CHUNKS)]
+    early = width * 5 // 8
+    spans = [(0, early), (early, width - early)]
     eighth, last = width // 8, width * 5 // 16
     parts = [(0, width - eighth - last), (width - eighth - last, last)]
     side = (width - eighth, eighth)
@@ -789,12 +789,14 @@
     loads["down_1"].wait()
 
     def project_down(start, size):
-        side = start // half
-        rows = pl.ds(width + side * ff, ff)
-        part[:, pl.ds(start, size)] = jnp.dot(
-            hidden[...], region[rows, pl.ds(start - side * half, size)],
-            preferred_element_type=F32,
-        ).astype(BF16)
+        wide = 512
+        for first in range(start, start + size, wide):
+            strip_side = first // half
+            rows = pl.ds(width + strip_side * ff, ff)
+            part[:, pl.ds(first, wide)] = jnp.dot(
+                hidden[...], region[rows, pl.ds(first - strip_side * half, wide)],
+                preferred_element_type=F32,
+            ).astype(BF16)
 
     Reduce(place, part, total, own_rows, spans, (s.rb_send, s.rb_recv), sums).run(project_down)
     own_member = place.tp * own_rows // batch

time: 161 us -> 159 us (0.988)
  Pallas kernels: 154 us -> 152 us
    pallas_call x1, Pallas kernels: 154 us -> 152 us  [fused_body(): pl.pallas_call(functools.partial(layer_kernel, lines, tuple(scratch)), ou...]
where the time goes in v3:
time: 159 us
  Pallas kernels  152 us (96%)
  local copies, waits for them, and re-layouts  4.88 us (3%)
    pallas_call x1, Pallas kernels, fused_body(): pl.pallas_call(functools.partial(layer_kernel, lines, tuple(scratch)), ou...  152 us
    unnamed x3, local copies, waits for them, and re-layouts  4.81 us

profile of v3, /device:TPU:0, one launch (start us, length us, event | category | flops | bytes accessed | tf_op | source)
XLA Modules:
  0.0 158.9 jit_solution(11274623789210091323)
XLA Ops:
  0.6 0.7 dynamic-slice_convert_fusion
  1.4 0.1 stack_broadcast_in_dim.2
  1.5 0.1 multiply_cosine_fusion
  1.6 0.1 maximum_bitcast_fusion
  1.7 0.6 pad_maximum_fusion.table
  2.3 1.3 copy.15.fast_hidden
  3.6 151.8 %shard_map.140 = (bf16[128,4096]{1,0:T(8,128)(2,1)}, f32[1,128]{1,0:T(1,128)}) custom-call(bf16[16,4096]{1,0:T(8,128)(2,1)} %stream.1, bf16[16,512,2048]{2,1,0:T(8,128)(2,1)} %cache.1, bf16[4096,384]{1,0:T(8,128)(2,1)} %w_qkv.1, bf16[256,4096]{1,0:T(8,128)(2,1)} %w_out.1, bf16[2,4096,896]{2,1,0:T(8,128)(2,1)} %w_gate_up.1, bf16[896,4096]{1,0:T(8,128)(2,1)} %w_down.1, ...), custom_call_target="tpu_custom_call" | custom-call | tf_op jit(solution)/shard_map/pallas_call | solution.py:1002
  155.4 2.3 %copy.18 = bf16[128,4096]{1,0:T(8,128)(2,1)} copy(bf16[128,4096]{1,0:T(8,128)(2,1)} %get-tuple-element.13) | data formatting | bytes 2097152
  157.7 1.2 copy.19
  (1 shorter events, 0.0 us)
